TPU v7x, 256 devices: a whole 4x4x8 slice. The times are simulated.
256 devices in a mesh: band: 4 (over x), col: 64 (over z, y, core).
Axes of the slice: x: 4, y: 4, z: 8, core: 2. Of those that a mesh axis runs over, the one named last changes fastest.
Arguments:
- obs_priors: float32 [80, 131072], P(None, ('band', 'col')), may hold values from -0.13258252 to 0.13258252
- innovation: float32 [131072], P(('band', 'col')), may hold values from -6 to 6
- obs_precision: float32 [131072], P(('band', 'col')), may hold values from 0.25 to 4
- tile_block: int32 [1024], P(('band', 'col')), may hold values from 0 to 3
- obs_count: int32 [256], P(('band', 'col')), may hold values from 128 to 512
- block_mask: int32 [4, 256], P(None, 'col'), may hold values 0 or 1
- prior_state_mean: float32 [256, 16, 1024], P('col', None, 'band'), may hold values from -6 to 6
- prior_state_deviation: float32 [256, 16, 80, 1024], P('col', None, None, 'band'), may hold values from -6 to 6
Outputs:
- posterior_mean: float32 [256, 16, 1024], P('col', None, 'band')
- analysis_perturb: float32 [256, 16, 80, 1024], P('col', None, None, 'band')
All inputs are finite; a program needn't handle non-finite values. No bound on the sum of `block_mask` on one device may be relied on, other than what follows from the above.
Results may differ from a plain program's by a relative error of at most 0.0001.
Values sent between devices are 32-bit elements; how exact they have to be, the bound alone decides.
No kernel may reach another device: no remote copies, remote signals or barrier semaphores. Data moves between devices by JAX's collectives and lax.ppermute only.
A program may use at most 64 MiB of HBM per device.

v0:
```python
import functools

import jax
import jax.numpy as jnp
from jax import lax
from jax.sharding import Mesh
from jax.sharding import PartitionSpec as P

COL = ("col_0", "col_1", "col_2")
BAND_COL = ("band", "col_0", "col_1", "col_2")


PRECISION_HIGH = lax.Precision.HIGHEST


def over_axes(value, axes):
    return functools.reduce(lax.psum, axes, value)


def passed_along(value, axis, by):
    length = lax.axis_size(axis)
    pairs = [(i, i + by) for i in range(length) if 0 <= i + by < length]
    return lax.ppermute(value, axis, pairs)


def broadcast(value, axis, root):
    return lax.dynamic_index_in_dim(lax.all_gather(value, axis), root, 0, keepdims=False)


def local(
    obs_priors,
    innovation,
    obs_precision,
    tile_block,
    obs_count,
    block_mask,
    prior_state_mean,
    prior_state_deviation,
):
    ensemble_members = obs_priors.shape[0]
    obs_rows = obs_priors.shape[1]
    tile_count = tile_block.shape[0]
    tile_rows = obs_rows // tile_count
    blocks = prior_state_mean.shape[0]
    priors = obs_priors.reshape(ensemble_members, tile_count, tile_rows)
    onehot = (tile_block[:, None] == jnp.arange(blocks, dtype=jnp.int32)[None, :]).astype(
        jnp.float32
    )
    live_rows = jnp.arange(obs_rows, dtype=jnp.int32) < obs_count[0]
    weights = jnp.where(live_rows, obs_precision, jnp.float32(0.0)).reshape(tile_count, tile_rows)
    innov_tiles = innovation.reshape(tile_count, tile_rows)
    identity = jnp.eye(ensemble_members, dtype=jnp.float32)
    band_count = lax.axis_size("band")
    my_band = lax.axis_index("band")

    def band_solve(turn_index, affine_update):

        def local_terms():
            tile_maps = jnp.einsum("tg,gkl->tkl", onehot, affine_update, precision=PRECISION_HIGH)
            updated = jnp.einsum("tkl,ktr->ltr", tile_maps, priors, precision=PRECISION_HIGH)
            spread = updated[:ensemble_members]
            departure = innov_tiles - updated[ensemble_members]
            curvature = jnp.einsum(
                "ltr,tr,mtr->lm", spread, weights, spread, precision=PRECISION_HIGH
            )
            projected = jnp.einsum(
                "ltr,tr->l", spread, weights * departure, precision=PRECISION_HIGH
            )
            return (curvature, projected)

        def no_terms():
            return (
                jnp.zeros((ensemble_members, ensemble_members), jnp.float32),
                jnp.zeros((ensemble_members,), jnp.float32),
            )

        partial_sums = lax.cond(my_band == turn_index, local_terms, no_terms)
        curvature, projected = jax.tree.map(lambda part: over_axes(part, COL), partial_sums)
        system = (ensemble_members - 1) * identity + curvature
        factor = jnp.linalg.cholesky(system)
        solved = jax.scipy.linalg.cho_solve(
            (factor, True), jnp.concatenate([projected[:, None], curvature], axis=1)
        )
        ensemble_transform = identity - 0.5 * solved[:, 1:]
        upper_part = jnp.concatenate([ensemble_transform, solved[:, :1]], axis=1)
        lower_part = jnp.concatenate(
            [jnp.zeros((1, ensemble_members), jnp.float32), jnp.ones((1, 1), jnp.float32)], axis=1
        )
        return jnp.concatenate([upper_part, lower_part], axis=0)

    def advance(affine_update, augmented, apply_flags):
        moved = jnp.einsum("gkl,lm->gkm", affine_update, augmented, precision=PRECISION_HIGH)
        return jnp.where(apply_flags[:, None, None], moved, affine_update)

    start = jnp.concatenate(
        [
            jnp.broadcast_to(identity, (blocks, ensemble_members, ensemble_members)),
            jnp.zeros((blocks, ensemble_members, 1), jnp.float32),
        ],
        axis=2,
    )

    def band_update(turn_index, affine_update):
        augmented = band_solve(turn_index, affine_update)
        apply_flags = (block_mask[turn_index] > 0) & (my_band == turn_index)
        return advance(affine_update, augmented, apply_flags)

    def relay_turn(turn_index, affine_update):
        updated = band_update(turn_index, affine_update)
        return passed_along(updated, "band", 1)

    affine_update = lax.fori_loop(0, band_count - 1, relay_turn, start)
    affine_update = band_update(band_count - 1, affine_update)
    affine_update = broadcast(affine_update, "band", band_count - 1)
    posterior_mean = prior_state_mean + jnp.einsum(
        "eu,evur->evr",
        affine_update[:, :, ensemble_members],
        prior_state_deviation,
        precision=PRECISION_HIGH,
    )
    analysis_perturb = jnp.einsum(
        "gkm,glkc->glmc",
        affine_update[:, :, :ensemble_members],
        prior_state_deviation,
        precision=PRECISION_HIGH,
    )
    return (posterior_mean, analysis_perturb)


def solution(mesh):
    torus = Mesh(
        mesh.devices.reshape(mesh.shape["band"], 8, 4, 2), ("band", "col_0", "col_1", "col_2")
    )
    placed = (
        P(None, BAND_COL),
        P(BAND_COL),
        P(BAND_COL),
        P(BAND_COL),
        P(BAND_COL),
        P(None, COL),
        P(COL, None, "band"),
        P(COL, None, None, "band"),
    )
    return jax.shard_map(
        local,
        mesh=torus,
        in_specs=placed,
        out_specs=(P(COL, None, "band"), P(COL, None, None, "band")),
        check_vma=False,
    )
```

profile of v0, /device:TPU:1, one launch (start us, length us, event | category | flops | bytes accessed | tf_op | source)
XLA Modules:
  0.0 327.1 jit_solution(5505786058018467794)
XLA Ops:
  1.3 0.7 select_bitcast_fusion
  2.1 0.9 copy_bitcast_fusion
  3.0 231.2 %while.15 = (s32[]{:T(128)}, f32[4,80,81]{2,1,0:T(8,128)S(1)}, s32[4,4]{1,0:T(4,128)}, s32[]{:T(128)}, f32[80,4,128]{2,0,1:T(8,128)S(1)}, /*index=5*/f32[4,128]{...) while((s32[]{:T(128)}, f32[4,80,81]{2,1,0:T(8,128)S(1)}, ...), condition=%wide.region_11.14_spmd.clone.clone, body=%wide.region_0.0_spmd.clone.clone.sunk | while | flops 118734904 | bytes 2493382 | solution.py:112
  3.1 0.8 fusion.86
  3.8 2.2 conditional.6
  3.8 0.4 fusion.5
  4.2 0.5 convolution_bitcast_fusion
  4.8 0.7 subtract_multiply_fusion
  5.7 0.3 convolution_bitcast_fusion.1
  6.1 27.0 %all-reduce.10 = (f32[80,80]{0,1:T(8,128)S(1)}, f32[80]{0:T(128)S(1)}) all-reduce(f32[80,80]{0,1:T(8,128)S(1)} %copy.81, f32[80]{0:T(128)S(1)} %get-tuple-element.361), channel_id=1, replica_groups=mesh['band'=4,'col_0'=8,'col_1'=4,'col_2'=2] {'col_0'}, use_global_device_ids=true, to_apply=%region_3.3 | all-reduce | flops 6480 | bytes 51840 | tf_op jit(solution)/shard_map/while/body/eval_jaxpr/psum | solution.py:17
  33.1 14.3 %all-reduce.11 = (f32[80,80]{0,1:T(8,128)S(1)}, f32[80]{0:T(128)S(1)}) all-reduce(f32[80,80]{0,1:T(8,128)S(1)} %get-tuple-element.362, f32[80]{0:T(128)S(1)} %get-tuple-element.363), channel_id=1, replica_groups=mesh['band'=4,'col_0'=8,'col_1'=4,'col_2'=2] {'col_1'}, use_global_device_ids=true, to_apply=%region_4.4 | all-reduce | flops 6480 | bytes 51840 | tf_op jit(solution)/shard_map/while/body/eval_jaxpr/psum | solution.py:17
  47.3 14.4 %all-reduce.12 = (f32[80,80]{0,1:T(8,128)S(1)}, f32[80,1]{0,1:T(1,128)S(1)}) all-reduce(f32[80,80]{0,1:T(8,128)S(1)} %get-tuple-element.364, f32[80,1]{0,1:T(1,128)S(1)} %bitcast.122), channel_id=1, replica_groups=mesh['band'=4,'col_0'=8,'col_1'=4,'col_2'=2] {'col_2'}, use_global_device_ids=true, to_apply=%region_5.5 | all-reduce | flops 6480 | bytes 51840 | tf_op jit(solution)/shard_map/while/body/eval_jaxpr/psum | solution.py:17
  61.8 7.3 %cholesky.117 = f32[80,80]{1,0:T(8,128)S(1)} custom-call(f32[80,80]{1,0:T(8,128)S(1)} %fusion.87), custom_call_target="Cholesky" | custom-call | tf_op jit(solution)/shard_map/while/body/eval_jaxpr/jit(cholesky)/cholesky | solution.py:80
  69.2 0.7 compare_reduce_fusion.3
  69.9 0.7 fusion.88
  70.6 6.1 %custom-call.11 = f32[1,80,80]{1,2,0:T(8,128)S(1)} custom-call(f32[1,80,80]{2,1,0:T(8,128)S(1)} %fusion.88), custom_call_target="InvertDiagBlocksLowerTriangular" | custom-call | tf_op jit(solution)/shard_map/while/body/eval_jaxpr/jit(_cho_solve)/triangular_solve | solution.py:81
  76.8 0.2 fusion.89
  77.0 0.3 fusion.90
  77.3 0.7 and_bitcast_fusion.3
  78.0 1.2 fusion.92
  79.2 1.3 collective-permute-start
  80.5 3.6 %collective-permute-done = f32[4,80,81]{2,1,0:T(8,128)S(1)} collective-permute-done((f32[4,80,81]{2,1,0:T(8,128)S(1)}, f32[4,80,81]{2,1,0:T(8,128)S(1)}, u32[]{:S(2)}, u32[]{:S(2)}) %collective-permute-start) | collective-permute-done | bytes 103712 | tf_op jit(solution)/shard_map/while/body/eval_jaxpr/ppermute | solution.py:23
  84.1 0.7 fusion.86
  84.9 20.5 %all-reduce.10 = (f32[80,80]{0,1:T(8,128)S(1)}, f32[80]{0:T(128)S(1)}) all-reduce(f32[80,80]{0,1:T(8,128)S(1)} %copy.81, f32[80]{0:T(128)S(1)} %get-tuple-element.361), channel_id=1, replica_groups=mesh['band'=4,'col_0'=8,'col_1'=4,'col_2'=2] {'col_0'}, use_global_device_ids=true, to_apply=%region_3.3 | all-reduce | flops 6480 | bytes 51840 | tf_op jit(solution)/shard_map/while/body/eval_jaxpr/psum | solution.py:17
  105.4 11.2 %all-reduce.11 = (f32[80,80]{0,1:T(8,128)S(1)}, f32[80]{0:T(128)S(1)}) all-reduce(f32[80,80]{0,1:T(8,128)S(1)} %get-tuple-element.362, f32[80]{0:T(128)S(1)} %get-tuple-element.363), channel_id=1, replica_groups=mesh['band'=4,'col_0'=8,'col_1'=4,'col_2'=2] {'col_1'}, use_global_device_ids=true, to_apply=%region_4.4 | all-reduce | flops 6480 | bytes 51840 | tf_op jit(solution)/shard_map/while/body/eval_jaxpr/psum | solution.py:17
  116.6 14.5 %all-reduce.12 = (f32[80,80]{0,1:T(8,128)S(1)}, f32[80,1]{0,1:T(1,128)S(1)}) all-reduce(f32[80,80]{0,1:T(8,128)S(1)} %get-tuple-element.364, f32[80,1]{0,1:T(1,128)S(1)} %bitcast.122), channel_id=1, replica_groups=mesh['band'=4,'col_0'=8,'col_1'=4,'col_2'=2] {'col_2'}, use_global_device_ids=true, to_apply=%region_5.5 | all-reduce | flops 6480 | bytes 51840 | tf_op jit(solution)/shard_map/while/body/eval_jaxpr/psum | solution.py:17
  131.3 7.3 %cholesky.117 = f32[80,80]{1,0:T(8,128)S(1)} custom-call(f32[80,80]{1,0:T(8,128)S(1)} %fusion.87), custom_call_target="Cholesky" | custom-call | tf_op jit(solution)/shard_map/while/body/eval_jaxpr/jit(cholesky)/cholesky | solution.py:80
  138.6 0.7 compare_reduce_fusion.3
  139.3 0.7 fusion.88
  140.0 6.1 %custom-call.11 = f32[1,80,80]{1,2,0:T(8,128)S(1)} custom-call(f32[1,80,80]{2,1,0:T(8,128)S(1)} %fusion.88), custom_call_target="InvertDiagBlocksLowerTriangular" | custom-call | tf_op jit(solution)/shard_map/while/body/eval_jaxpr/jit(_cho_solve)/triangular_solve | solution.py:81
  146.4 0.3 fusion.90
  146.7 0.7 and_bitcast_fusion.3
  147.4 1.2 fusion.92
  148.6 6.3 %collective-permute-start = (f32[4,80,81]{2,1,0:T(8,128)S(1)}, f32[4,80,81]{2,1,0:T(8,128)S(1)}, u32[]{:S(2)}, u32[]{:S(2)}) collective-permute-start(f32[4,80,81]{2,1,0:T(8,128)S(1)} %fusion.92), channel_id=1, source_target_pairs={{0,64},{64,128},{128,192},{1,65},{65,129},{129,193},{2,66},{66,130... | collective-permute-start | bytes 311048 | tf_op jit(solution)/shard_map/while/body/eval_jaxpr/ppermute | solution.py:23
  154.9 3.3 %collective-permute-done = f32[4,80,81]{2,1,0:T(8,128)S(1)} collective-permute-done((f32[4,80,81]{2,1,0:T(8,128)S(1)}, f32[4,80,81]{2,1,0:T(8,128)S(1)}, u32[]{:S(2)}, u32[]{:S(2)}) %collective-permute-start) | collective-permute-done | bytes 103712 | tf_op jit(solution)/shard_map/while/body/eval_jaxpr/ppermute | solution.py:23
  158.2 0.7 fusion.86
  159.1 22.1 %all-reduce.10 = (f32[80,80]{0,1:T(8,128)S(1)}, f32[80]{0:T(128)S(1)}) all-reduce(f32[80,80]{0,1:T(8,128)S(1)} %copy.81, f32[80]{0:T(128)S(1)} %get-tuple-element.361), channel_id=1, replica_groups=mesh['band'=4,'col_0'=8,'col_1'=4,'col_2'=2] {'col_0'}, use_global_device_ids=true, to_apply=%region_3.3 | all-reduce | flops 6480 | bytes 51840 | tf_op jit(solution)/shard_map/while/body/eval_jaxpr/psum | solution.py:17
  181.2 12.8 %all-reduce.11 = (f32[80,80]{0,1:T(8,128)S(1)}, f32[80]{0:T(128)S(1)}) all-reduce(f32[80,80]{0,1:T(8,128)S(1)} %get-tuple-element.362, f32[80]{0:T(128)S(1)} %get-tuple-element.363), channel_id=1, replica_groups=mesh['band'=4,'col_0'=8,'col_1'=4,'col_2'=2] {'col_1'}, use_global_device_ids=true, to_apply=%region_4.4 | all-reduce | flops 6480 | bytes 51840 | tf_op jit(solution)/shard_map/while/body/eval_jaxpr/psum | solution.py:17
  193.9 15.4 %all-reduce.12 = (f32[80,80]{0,1:T(8,128)S(1)}, f32[80,1]{0,1:T(1,128)S(1)}) all-reduce(f32[80,80]{0,1:T(8,128)S(1)} %get-tuple-element.364, f32[80,1]{0,1:T(1,128)S(1)} %bitcast.122), channel_id=1, replica_groups=mesh['band'=4,'col_0'=8,'col_1'=4,'col_2'=2] {'col_2'}, use_global_device_ids=true, to_apply=%region_5.5 | all-reduce | flops 6480 | bytes 51840 | tf_op jit(solution)/shard_map/while/body/eval_jaxpr/psum | solution.py:17
  209.4 7.3 %cholesky.117 = f32[80,80]{1,0:T(8,128)S(1)} custom-call(f32[80,80]{1,0:T(8,128)S(1)} %fusion.87), custom_call_target="Cholesky" | custom-call | tf_op jit(solution)/shard_map/while/body/eval_jaxpr/jit(cholesky)/cholesky | solution.py:80
  216.8 0.7 compare_reduce_fusion.3
  217.5 0.7 fusion.88
  218.2 6.1 %custom-call.11 = f32[1,80,80]{1,2,0:T(8,128)S(1)} custom-call(f32[1,80,80]{2,1,0:T(8,128)S(1)} %fusion.88), custom_call_target="InvertDiagBlocksLowerTriangular" | custom-call | tf_op jit(solution)/shard_map/while/body/eval_jaxpr/jit(_cho_solve)/triangular_solve | solution.py:81
  224.3 0.2 fusion.89
  224.6 0.3 fusion.90
  224.9 0.7 and_bitcast_fusion.3
  225.6 1.2 fusion.92
  226.8 4.1 %collective-permute-start = (f32[4,80,81]{2,1,0:T(8,128)S(1)}, f32[4,80,81]{2,1,0:T(8,128)S(1)}, u32[]{:S(2)}, u32[]{:S(2)}) collective-permute-start(f32[4,80,81]{2,1,0:T(8,128)S(1)} %fusion.92), channel_id=1, source_target_pairs={{0,64},{64,128},{128,192},{1,65},{65,129},{129,193},{2,66},{66,130... | collective-permute-start | bytes 311048 | tf_op jit(solution)/shard_map/while/body/eval_jaxpr/ppermute | solution.py:23
  230.9 3.3 %collective-permute-done = f32[4,80,81]{2,1,0:T(8,128)S(1)} collective-permute-done((f32[4,80,81]{2,1,0:T(8,128)S(1)}, f32[4,80,81]{2,1,0:T(8,128)S(1)}, u32[]{:S(2)}, u32[]{:S(2)}) %collective-permute-start) | collective-permute-done | bytes 103712 | tf_op jit(solution)/shard_map/while/body/eval_jaxpr/ppermute | solution.py:23
  234.3 0.7 fusion.54
  235.1 20.8 %all-reduce.4 = (f32[80,80]{0,1:T(8,128)S(1)}, f32[80]{0:T(128)S(1)}) all-reduce(f32[80,80]{0,1:T(8,128)S(1)} %copy.48, f32[80]{0:T(128)S(1)} %get-tuple-element.197), channel_id=1, replica_groups=mesh['band'=4,'col_0'=8,'col_1'=4,'col_2'=2] {'col_0'}, use_global_device_ids=true, to_apply=%region_14.17 | all-reduce | flops 6480 | bytes 51840 | tf_op jit(solution)/shard_map/psum | solution.py:17
  255.9 11.2 %all-reduce.5 = (f32[80,80]{0,1:T(8,128)S(1)}, f32[80]{0:T(128)S(1)}) all-reduce(f32[80,80]{0,1:T(8,128)S(1)} %get-tuple-element.297, f32[80]{0:T(128)S(1)} %get-tuple-element.298), channel_id=1, replica_groups=mesh['band'=4,'col_0'=8,'col_1'=4,'col_2'=2] {'col_1'}, use_global_device_ids=true, to_apply=%region_15.18 | all-reduce | flops 6480 | bytes 51840 | tf_op jit(solution)/shard_map/psum | solution.py:17
  267.1 14.6 %all-reduce.6 = (f32[80,80]{0,1:T(8,128)S(1)}, f32[80,1]{0,1:T(1,128)S(1)}) all-reduce(f32[80,80]{0,1:T(8,128)S(1)} %get-tuple-element.299, f32[80,1]{0,1:T(1,128)S(1)} %bitcast.126), channel_id=1, replica_groups=mesh['band'=4,'col_0'=8,'col_1'=4,'col_2'=2] {'col_2'}, use_global_device_ids=true, to_apply=%region_16.19 | all-reduce | flops 6480 | bytes 51840 | tf_op jit(solution)/shard_map/psum | solution.py:17
  281.8 7.3 %cholesky.55 = f32[80,80]{1,0:T(8,128)S(1)} custom-call(f32[80,80]{1,0:T(8,128)S(1)} %fusion.52), custom_call_target="Cholesky" | custom-call | tf_op jit(solution)/shard_map/jit(cholesky)/cholesky | solution.py:80
  289.1 0.6 compare_reduce_fusion.1
  289.8 0.7 fusion.47
  290.4 6.1 %custom-call.9 = f32[1,80,80]{1,2,0:T(8,128)S(1)} custom-call(f32[1,80,80]{2,1,0:T(8,128)S(1)} %fusion.47), custom_call_target="InvertDiagBlocksLowerTriangular" | custom-call | tf_op jit(solution)/shard_map/jit(_cho_solve)/triangular_solve | solution.py:81
  296.8 0.3 fusion.49
  297.1 0.7 and_bitcast_fusion.1
  297.8 1.1 convolution_select_fusion
  299.0 15.1 %all-gather = f32[16,80,81]{2,1,0:T(8,128)S(1)} all-gather(f32[4,80,81]{2,1,0:T(8,128)S(1)} %convolution_select_fusion), channel_id=2, replica_groups=mesh['band'=4,'col_0'=8,'col_1'=4,'col_2'=2] {'band'}, dimensions={0}, use_global_device_ids=true | all-gather | bytes 518400 | tf_op jit(solution)/shard_map/all_gather | solution.py:27
  314.1 9.6 %convolution_bitcast_fusion.7 = f32[4,16,80,256]{3,2,1,0:T(8,128)} fusion(f32[4,16,80,256]{3,2,1,0:T(8,128)} %param.24, f32[16,80,81]{2,1,0:T(8,128)S(1)} %all-gather), kind=kOutput, calls=%fused_computation.58 | convolution fusion | flops 1258291200 | bytes 10649600 | tf_op jit(solution)/shard_map/gkm,glkc->glmc/dot_general | solution.py:121
  323.9 2.6 fusion.57
  326.5 0.6 bitcast_add_fusion.1
  (56 shorter events, 2.1 us)
Async XLA Ops:
  3.0 231.2 %copy-start = (f32[80,512]{1,0:T(8,128)S(1)}, f32[80,512]{1,0:T(8,128)}, u32[]{:S(2)}) copy-start(f32[80,512]{1,0:T(8,128)} %param.17) | copy-start | bytes 491524
  79.2 4.9 %collective-permute-start = (f32[4,80,81]{2,1,0:T(8,128)S(1)}, f32[4,80,81]{2,1,0:T(8,128)S(1)}, u32[]{:S(2)}, u32[]{:S(2)}) collective-permute-start(f32[4,80,81]{2,1,0:T(8,128)S(1)} %fusion.92), channel_id=1, source_target_pairs={{0,64},{64,128},{128,192},{1,65},{65,129},{129,193},{2,66},{66,130... | collective-permute-start | bytes 311048 | tf_op jit(solution)/shard_map/while/body/eval_jaxpr/ppermute | solution.py:23
  148.6 9.6 %collective-permute-start = (f32[4,80,81]{2,1,0:T(8,128)S(1)}, f32[4,80,81]{2,1,0:T(8,128)S(1)}, u32[]{:S(2)}, u32[]{:S(2)}) collective-permute-start(f32[4,80,81]{2,1,0:T(8,128)S(1)} %fusion.92), channel_id=1, source_target_pairs={{0,64},{64,128},{128,192},{1,65},{65,129},{129,193},{2,66},{66,130... | collective-permute-start | bytes 311048 | tf_op jit(solution)/shard_map/while/body/eval_jaxpr/ppermute | solution.py:23
  226.8 7.5 %collective-permute-start = (f32[4,80,81]{2,1,0:T(8,128)S(1)}, f32[4,80,81]{2,1,0:T(8,128)S(1)}, u32[]{:S(2)}, u32[]{:S(2)}) collective-permute-start(f32[4,80,81]{2,1,0:T(8,128)S(1)} %fusion.92), channel_id=1, source_target_pairs={{0,64},{64,128},{128,192},{1,65},{65,129},{129,193},{2,66},{66,130... | collective-permute-start | bytes 311048 | tf_op jit(solution)/shard_map/while/body/eval_jaxpr/ppermute | solution.py:23
  299.0 24.9 %slice-start = ((s8[5242880]{0:T(1024)(128)(4,1)}), s8[4194304]{0:T(1024)(128)(4,1)S(1)}, s32[]{:S(2)}) async-start(s8[5242880]{0:T(1024)(128)(4,1)} %bitcast.117), calls=%async_computation | async-start | bytes 8388608
  314.1 9.8 %slice-start.1 = ((s8[5242880]{0:T(1024)(128)(4,1)}), s8[1048576]{0:T(1024)(128)(4,1)S(1)}, s32[]{:S(2)}) async-start(s8[5242880]{0:T(1024)(128)(4,1)} %bitcast.117), calls=%async_computation.1 | async-start | bytes 2097152
  323.6 2.8 copy-start.1
where the time goes:
time: 329 us; the launch traced here: 327 us
  blocking collectives  214 us (65%)
  other arithmetic  67.3 us (20%)
  matrix products  20.3 us (6%)
  starting transfers between devices  11.7 us (4%)
  waiting for transfers between devices  10.3 us (3%)
    psum x12, blocking collectives, over_axes(): return functools.reduce(lax.psum, axes, value)  199 us
    another operation x12, other arithmetic, band_solve(): factor = jnp.linalg.cholesky(system)  32.2 us
    another operation x8, other arithmetic, band_solve(): jax.scipy.linalg.cho_solve((factor, True), jnp.concatenate([projected[:,...  27.3 us
    all_gather x1, blocking collectives, broadcast(): lax.all_gather(value, axis)  15.1 us
    ppermute x3, starting transfers between devices, passed_along(): return lax.ppermute(value, axis, pairs)  11.7 us
    ppermute x3, waiting for transfers between devices, passed_along(): return lax.ppermute(value, axis, pairs)  10.3 us
    dot_general x1, matrix products, local(): jnp.einsum('gkm,glkc->glmc', affine_update[:, :, :ensemble_members], prio...  9.58 us
  transfers between devices with their start and end apart: 3, of which 3 were waited for; matrix products, arithmetic and copies ran while one was open for 0% of the time, Pallas kernels for 0%

commit v1 on v0

v1 whole, which is shorter than its diff:
```python
import functools

import jax
import jax.numpy as jnp
from jax import lax
from jax.experimental import pallas as pl
from jax.experimental.pallas import tpu as pltpu
from jax.sharding import Mesh
from jax.sharding import PartitionSpec as P

COL = ("col_0", "col_1", "col_2")
BAND_COL = ("band", "col_0", "col_1", "col_2")
HIGHEST = lax.Precision.HIGHEST
LANES = 128
SUB = 8


def lane_of(shape):
    return lax.broadcasted_iota(jnp.int32, shape, 1)


def row_of(shape):
    return lax.broadcasted_iota(jnp.int32, shape, 0)


def matmul(a, b, dims=((1,), (0,))):
    return lax.dot_general(
        a, b, (dims, ((), ())), precision=HIGHEST, preferred_element_type=jnp.float32
    )


def statistics_kernel(
    members,
    band_ref,
    tile_block_ref,
    obs_count_ref,
    block_mask_ref,
    priors_ref,
    innovation_ref,
    precision_ref,
    out_ref,
):
    tiles = tile_block_ref.shape[0]
    tile_rows = priors_ref.shape[1] // tiles
    bands = block_mask_ref.shape[0]
    pairs = 1 << (bands - 2)
    band = band_ref[0]
    count = obs_count_ref[0]
    lane = lane_of((members, LANES))
    row = row_of((members, LANES))
    moments = []
    history = []
    for t in range(tiles):
        cols = pl.ds(t * tile_rows, tile_rows)
        x = priors_ref[:, cols]
        live = (lane_of((1, tile_rows)) + t * tile_rows) < count
        r = jnp.where(live, precision_ref[:, cols], jnp.float32(0.0))
        z = jnp.concatenate(
            [
                x,
                jnp.where(
                    row_of((LANES - members, tile_rows)) == 0, -innovation_ref[:, cols], 0.0
                ),
            ],
            axis=0,
        )
        moments.append(matmul(x * r, z, ((1,), (1,))))
        block = tile_block_ref[t]
        code = jnp.int32(0)
        for j in range(bands - 1):
            applied = jnp.where((block_mask_ref[j, block] > 0) & (j < band), 1 << j, 0)
            code = code + applied
        history.append(code)

    def of_history(s):
        total = jnp.zeros((members, LANES), jnp.float32)
        for t in range(tiles):
            total = total + moments[t] * jnp.where(history[t] == s, 1.0, 0.0)
        return total

    for p in range(pairs):
        even = of_history(2 * p)
        odd = of_history(2 * p + 1)
        packed = jnp.where(lane > row, pltpu.roll(odd, 1, 1), even)
        packed = jnp.where(lane == members + 2, pltpu.roll(even, 2, 1), packed)
        packed = jnp.where(lane > members + 2, 0.0, packed)
        out_ref[pl.ds(p * members, members), :] = packed


def unpack(packed, scratch, members):
    lane = lane_of((members, LANES))
    row = row_of((members, LANES))
    square = jnp.concatenate(
        [packed, jnp.zeros((LANES - members, LANES), jnp.float32)], axis=0
    )
    scratch[...] = square.T
    even = jnp.where(lane <= row, packed, scratch[pl.ds(0, members), :])
    even = jnp.where(lane == members, pltpu.roll(packed, LANES - 2, 1), even)
    even = jnp.where(lane > members, 0.0, even)
    odd = jnp.where(lane >= row, pltpu.roll(packed, LANES - 1, 1), scratch[pl.ds(1, members), :])
    odd = jnp.where(lane > members, 0.0, odd)
    return even, odd


def inverse_and_solution(system, members):
    blocks = members // SUB
    rows = [system[SUB * i : SUB * (i + 1), :] for i in range(blocks)]
    lane = lane_of((SUB, LANES))
    sub = row_of((SUB, LANES))
    for k in range(blocks):
        base = SUB * k
        inside = (lane >= base) & (lane < base + SUB)
        pivot = rows[k]
        spread = [
            jnp.broadcast_to(pivot[:, base + j : base + j + 1], (SUB, LANES)) for j in range(SUB)
        ]
        pivot = jnp.where(inside, jnp.where(lane - base == sub, 1.0, 0.0), pivot)
        for i in range(SUB):
            here = sub == i
            scale = 1.0 / jnp.broadcast_to(spread[i][i : i + 1, :], (SUB, LANES))
            own = jnp.broadcast_to(pivot[i : i + 1, :], (SUB, LANES)) * scale
            factor = spread[i]
            pivot = jnp.where(here, own, pivot - factor * own)
            for j in range(i + 1, SUB):
                other = jnp.broadcast_to(spread[j][i : i + 1, :], (SUB, LANES)) * scale
                spread[j] = jnp.where(here, other, spread[j] - factor * other)
        fresh = [jnp.broadcast_to(pivot[i : i + 1, :], (SUB, LANES)) for i in range(SUB)]
        order = [(k + 1 + m) % blocks for m in range(blocks - 1)]
        for m in order:
            held = rows[m]
            total = jnp.where(inside, 0.0, held)
            for i in range(SUB):
                total = total - held[:, base + i : base + i + 1] * fresh[i]
            rows[m] = total
        rows[k] = pivot
    return jnp.concatenate(rows, axis=0)


def analysis_kernel(
    members,
    block_mask_ref,
    gathered_ref,
    mean_ref,
    deviation_hbm,
    mean_out_ref,
    perturb_hbm,
    deviation,
    perturb,
    maps,
    flip,
    right,
    lhs,
    in_sem,
    out_sem,
):
    bands, groups = block_mask_ref.shape
    levels = mean_ref.shape[1]
    columns = mean_ref.shape[2]
    pairs = 1 << (bands - 2)
    lane = lane_of((members, LANES))
    row = row_of((members, LANES))
    loads = [
        pltpu.make_async_copy(deviation_hbm.at[g], deviation.at[g], in_sem.at[g])
        for g in range(groups)
    ]
    for load in loads:
        load.start()

    by_band = []
    for b in range(bands):
        found = []
        for p in range(max(1, (1 << b) // 2)):
            packed = gathered_ref[pl.ds((b * pairs + p) * members, members), :]
            even, odd = unpack(packed, flip, members)
            found.append(even)
            if b > 0:
                found.append(odd)
        by_band.append(found)

    diagonal = lane == row
    current = [jnp.where(diagonal, 1.0, 0.0) for _ in range(groups)]
    lower = jnp.where(
        (row_of((LANES - members, LANES)) == 0) & (lane_of((LANES - members, LANES)) == members),
        1.0,
        0.0,
    )
    for b in range(bands):
        moment = by_band[b][0]
        system = jnp.where(
            lane == members, -moment, moment + jnp.where(diagonal, members - 1.0, 0.0)
        )
        solved = inverse_and_solution(system, members)
        transform = jnp.where(
            lane < members,
            jnp.where(diagonal, 0.5, 0.0) + (0.5 * (members - 1)) * solved,
            jnp.where(lane == members, solved, 0.0),
        )
        augmented = jnp.concatenate([transform, lower], axis=0)
        for later in range(b + 1, bands):
            held = by_band[later]
            merged = []
            for s in range(0, len(held), 2):
                moved = matmul(held[s + 1], augmented)
                moved = matmul(transform, moved, ((0,), (0,)))[:members, :]
                merged.append(held[s] + moved)
            by_band[later] = merged
        for g in range(groups):
            moved = transform if b == 0 else matmul(current[g], augmented)
            current[g] = jnp.where(block_mask_ref[b, g] > 0, moved, current[g])

    for g in range(groups):
        high = current[g].astype(jnp.bfloat16).astype(jnp.float32)
        low = (current[g] - high).astype(jnp.bfloat16).astype(jnp.float32)
        stack = jnp.concatenate(
            [high, low, high, jnp.zeros((2 * LANES - 3 * members, LANES), jnp.float32)], axis=0
        )
        lhs[g] = stack.T.astype(jnp.bfloat16)

    stores = []
    zero = jnp.zeros((2 * LANES - 3 * members, columns), jnp.bfloat16)
    for g in range(groups):
        loads[g].wait()

        def one_level(l, carry):
            d = deviation[g, l]
            high = d.astype(jnp.bfloat16)
            low = (d - high.astype(jnp.float32)).astype(jnp.bfloat16)
            rhs = jnp.concatenate([high, high, low, zero], axis=0)
            product = jnp.dot(lhs[g], rhs, preferred_element_type=jnp.float32)
            perturb[g, l] = product[:members]
            mean_out_ref[g, pl.ds(l, 1), :] = (
                mean_ref[g, pl.ds(l, 1), :] + product[members : members + 1]
            )
            return carry

        lax.fori_loop(0, levels, one_level, 0, unroll=4)
        store = pltpu.make_async_copy(perturb.at[g], perturb_hbm.at[g], out_sem.at[g])
        store.start()
        stores.append(store)
    for store in stores:
        store.wait()


def local(
    obs_priors,
    innovation,
    obs_precision,
    tile_block,
    obs_count,
    block_mask,
    prior_state_mean,
    prior_state_deviation,
):
    members = obs_priors.shape[0]
    groups, levels, columns = prior_state_mean.shape
    bands = block_mask.shape[0]
    pairs = 1 << (bands - 2)
    parts = lax.axis_size(COL)
    everyone = lax.axis_size(BAND_COL)
    vmem = pl.BlockSpec(memory_space=pltpu.VMEM)
    smem = pl.BlockSpec(memory_space=pltpu.SMEM)
    hbm = pl.BlockSpec(memory_space=pl.ANY)
    my_band = lax.axis_index("band").astype(jnp.int32).reshape(1)
    packed = pl.pallas_call(
        functools.partial(statistics_kernel, members),
        out_shape=jax.ShapeDtypeStruct((pairs * members, LANES), jnp.float32),
        in_specs=[smem] * 4 + [vmem] * 3,
        out_specs=vmem,
    )(
        my_band,
        tile_block,
        obs_count,
        block_mask,
        obs_priors,
        innovation.reshape(1, -1),
        obs_precision.reshape(1, -1),
    )
    share = pairs * members * LANES // parts
    received = lax.all_to_all(packed.reshape(parts, share), COL, 0, 0, tiled=True)
    summed = jnp.sum(received, axis=0, keepdims=True)
    gathered = lax.all_to_all(
        jnp.broadcast_to(summed, (everyone, share)), BAND_COL, 0, 0, tiled=True
    )
    gathered = gathered.reshape(bands * pairs * members, LANES)
    return pl.pallas_call(
        functools.partial(analysis_kernel, members),
        out_shape=(
            jax.ShapeDtypeStruct(prior_state_mean.shape, jnp.float32),
            jax.ShapeDtypeStruct(prior_state_deviation.shape, jnp.float32),
        ),
        in_specs=[smem, vmem, vmem, hbm],
        out_specs=(vmem, hbm),
        scratch_shapes=[
            pltpu.VMEM(prior_state_deviation.shape, jnp.float32),
            pltpu.VMEM(prior_state_deviation.shape, jnp.float32),
            pltpu.VMEM((groups, members, LANES), jnp.float32),
            pltpu.VMEM((LANES, LANES), jnp.float32),
            pltpu.VMEM((LANES, LANES), jnp.float32),
            pltpu.VMEM((groups, LANES, 2 * LANES), jnp.bfloat16),
            pltpu.SemaphoreType.DMA((groups,)),
            pltpu.SemaphoreType.DMA((groups,)),
        ],
    )(block_mask, gathered, prior_state_mean, prior_state_deviation)


def solution(mesh):
    cols = mesh.shape["col"]
    shape = (mesh.shape["band"], cols // 8, 4, 2) if cols % 8 == 0 else (mesh.shape["band"], 1, 1, cols)
    torus = Mesh(mesh.devices.reshape(shape), BAND_COL)
    placed = (
        P(None, BAND_COL),
        P(BAND_COL),
        P(BAND_COL),
        P(BAND_COL),
        P(BAND_COL),
        P(None, COL),
        P(COL, None, "band"),
        P(COL, None, None, "band"),
    )
    return jax.shard_map(
        local,
        mesh=torus,
        in_specs=placed,
        out_specs=(P(COL, None, "band"), P(COL, None, None, "band")),
        check_vma=False,
    )
```

time: 329 us -> 78.2 us (0.24)
  blocking collectives: 214 us -> 53.9 us
  other arithmetic: 67.3 us -> 0.13 us
  Pallas kernels: 0 us -> 22.1 us
  matrix products: 20.3 us -> 0 us
  starting transfers between devices: 11.7 us -> 0 us
  waiting for transfers between devices: 10.3 us -> 0 us
    psum x12 -> x0, blocking collectives: 199 us -> none  [over_axes(): return functools.reduce(lax.psum, axes, value)]
    another operation x20 -> x0, other arithmetic: 59.4 us -> none  [the longest x12 32.2 us: band_solve(): factor = jnp.linalg.cholesky(system)]
    all_to_all x0 -> x2, blocking collectives: none -> 53.9 us  [the longest x1 29.1 us: local(): lax.all_to_all(jnp.broadcast_to(summed, (everyone, share)), BAND_COL, 0,...]
    pallas_call x0 -> x2, Pallas kernels: none -> 22.1 us  [the longest x1 19.9 us: local(): pl.pallas_call(functools.partial(analysis_kernel, members), out_shape=(ja...]
    dot_general x10 -> x0, matrix products: 18.2 us -> none  [the longest x1 9.58 us: local(): jnp.einsum('gkm,glkc->glmc', affine_update[:, :, :ensemble_members], prio...]
    all_gather x1 -> x0, blocking collectives: 15.1 us -> none  [broadcast(): lax.all_gather(value, axis)]
    ppermute x3 -> x0, starting transfers between devices: 11.7 us -> none  [passed_along(): return lax.ppermute(value, axis, pairs)]
    ppermute x3 -> x0, waiting for transfers between devices: 10.3 us -> none  [passed_along(): return lax.ppermute(value, axis, pairs)]
  transfers between devices with their start and end apart: 3 -> 0, of which waited for: 3 -> 0; matrix products, arithmetic and copies ran while one was open for 0% -> 0% of each run, Pallas kernels for 0% -> 0%
where the time goes in v1:
time: 78.2 us; the launch traced here: 77.9 us
  blocking collectives  53.9 us (69%)
  Pallas kernels  22.1 us (28%)
  between operations  1.45 us (2%)
    all_to_all x1, blocking collectives, local(): lax.all_to_all(jnp.broadcast_to(summed, (everyone, share)), BAND_COL, 0,...  29.1 us
    all_to_all x1, blocking collectives, local(): lax.all_to_all(packed.reshape(parts, share), COL, 0, 0, tiled=True)  24.8 us
    pallas_call x1, Pallas kernels, local(): pl.pallas_call(functools.partial(analysis_kernel, members), out_shape=(ja...  19.9 us
    pallas_call x1, Pallas kernels, local(): pl.pallas_call(functools.partial(statistics_kernel, members), out_shape=j...  2.18 us

profile of v1, /device:TPU:1, one launch (start us, length us, event | category | flops | bytes accessed | tf_op | source)
XLA Modules:
  0.0 77.9 jit_solution(986522395002856327)
XLA Ops:
  1.3 2.2 %shard_map.95 = f32[320,128]{1,0:T(8,128)} custom-call(s32[1]{0:T(128)} %bitcast.band_ref, s32[4]{0:T(128)} %tile_block_ref.1, s32[1]{0:T(128)S(6)} %copy.11.obs_count_ref, s32[4,4]{1,0:T(4,128)} %block_mask_ref.3, f32[80,512]{1,0:T(8,128)} %priors_ref.1, f32[1,512]{1,0:T(1,128)} %bitcast.7, f32[1,512]{1,0:T(1,128)} %bitcast.8), custom_call_target="tpu_custom_call" | custom-call | tf_op jit(solution)/shard_map/pallas_call | solution.py:264
  3.5 24.8 %all_to_all.15 = f32[64,1,640]{2,1,0:T(1,128)S(1)} all-to-all(f32[64,1,640]{2,1,0:T(1,128)} %bitcast.6), channel_id=1, replica_groups=mesh['band'=4,'col_0'=8,'col_1'=4,'col_2'=2] {'col_0','col_1','col_2'}, dimensions={0} | all-to-all | bytes 327680 | tf_op jit(solution)/shard_map/all_to_all | solution.py:279
  28.3 0.1 reduce_sum.9
  28.4 0.3 broadcast_in_dim.2
  28.7 29.1 %all_to_all.16 = f32[256,1,640]{2,1,0:T(1,128)} all-to-all(f32[256,1,640]{2,1,0:T(1,128)S(1)} %broadcast_in_dim.2), channel_id=1, replica_groups=mesh['band'=4,'col_0'=8,'col_1'=4,'col_2'=2] {'band','col_0','col_1','co..., dimensions={0} | all-to-all | bytes 1310720 | tf_op jit(solution)/shard_map/all_to_all | solution.py:281
  57.9 19.9 %shard_map.96 = (f32[4,16,256]{2,1,0:T(8,128)}, f32[4,16,80,256]{3,2,1,0:T(8,128)}) custom-call(s32[4,4]{1,0:T(4,128)} %block_mask_ref.3, f32[1280,128]{1,0:T(8,128)} %bitcast.5, f32[4,16,256]{2,1,0:T(8,128)} %mean_ref.1, f32[4,16,80,256]{3,2,1,0:T(8,128)} %deviation_hbm.1), custom_call_target="tpu_custom_call" | custom-call | tf_op jit(solution)/shard_map/pallas_call | solution.py:285

commit v2 on v1

--- a/solution.py
+++ b/solution.py
@@ -10,6 +10,9 @@
 
 COL = ("col_0", "col_1", "col_2")
 BAND_COL = ("band", "col_0", "col_1", "col_2")
+CORE = "col_2"
+CORE_FIRST = ("col_2", "col_0", "col_1")
+SAME_CORE = ("band", "col_0", "col_1")
 HIGHEST = lax.Precision.HIGHEST
 LANES = 128
 SUB = 8
@@ -102,7 +105,7 @@
     return even, odd
 
 
-def inverse_and_solution(system, members):
+def inverse_and_solution(system, nothing, members):
     blocks = members // SUB
     rows = [system[SUB * i : SUB * (i + 1), :] for i in range(blocks)]
     lane = lane_of((SUB, LANES))
@@ -112,7 +115,8 @@
         inside = (lane >= base) & (lane < base + SUB)
         pivot = rows[k]
         spread = [
-            jnp.broadcast_to(pivot[:, base + j : base + j + 1], (SUB, LANES)) for j in range(SUB)
+            nothing + jnp.broadcast_to(pivot[:, base + j : base + j + 1], (SUB, LANES))
+            for j in range(SUB)
         ]
         pivot = jnp.where(inside, jnp.where(lane - base == sub, 1.0, 0.0), pivot)
         for i in range(SUB):
@@ -146,9 +150,8 @@
     perturb_hbm,
     deviation,
     perturb,
-    maps,
+    nothing,
     flip,
-    right,
     lhs,
     in_sem,
     out_sem,
@@ -156,6 +159,7 @@
     bands, groups = block_mask_ref.shape
     levels = mean_ref.shape[1]
     columns = mean_ref.shape[2]
+    cores = gathered_ref.shape[0]
     pairs = 1 << (bands - 2)
     lane = lane_of((members, LANES))
     row = row_of((members, LANES))
@@ -165,12 +169,15 @@
     ]
     for load in loads:
         load.start()
+    nothing[...] = jnp.zeros_like(nothing)
 
     by_band = []
     for b in range(bands):
         found = []
         for p in range(max(1, (1 << b) // 2)):
-            packed = gathered_ref[pl.ds((b * pairs + p) * members, members), :]
+            half = pairs // cores
+            at = (b * half + p % half) * members
+            packed = gathered_ref[p // half, pl.ds(at, members), :]
             even, odd = unpack(packed, flip, members)
             found.append(even)
             if b > 0:
@@ -189,7 +196,7 @@
         system = jnp.where(
             lane == members, -moment, moment + jnp.where(diagonal, members - 1.0, 0.0)
         )
-        solved = inverse_and_solution(system, members)
+        solved = inverse_and_solution(system, nothing[...], members)
         transform = jnp.where(
             lane < members,
             jnp.where(diagonal, 0.5, 0.0) + (0.5 * (members - 1)) * solved,
@@ -256,7 +263,7 @@
     bands = block_mask.shape[0]
     pairs = 1 << (bands - 2)
     parts = lax.axis_size(COL)
-    everyone = lax.axis_size(BAND_COL)
+    everyone = lax.axis_size(SAME_CORE)
     vmem = pl.BlockSpec(memory_space=pltpu.VMEM)
     smem = pl.BlockSpec(memory_space=pltpu.SMEM)
     hbm = pl.BlockSpec(memory_space=pl.ANY)
@@ -276,12 +283,12 @@
         obs_precision.reshape(1, -1),
     )
     share = pairs * members * LANES // parts
-    received = lax.all_to_all(packed.reshape(parts, share), COL, 0, 0, tiled=True)
+    received = lax.all_to_all(packed.reshape(parts, share), CORE_FIRST, 0, 0, tiled=True)
     summed = jnp.sum(received, axis=0, keepdims=True)
-    gathered = lax.all_to_all(
-        jnp.broadcast_to(summed, (everyone, share)), BAND_COL, 0, 0, tiled=True
-    )
-    gathered = gathered.reshape(bands * pairs * members, LANES)
+    copies = jnp.broadcast_to(summed, (everyone, share))
+    own_half = lax.all_to_all(copies, SAME_CORE, 0, 0, tiled=True)
+    own_half = own_half.reshape(-1, LANES)
+    gathered = lax.all_gather(own_half, CORE, axis=0, tiled=False)
     return pl.pallas_call(
         functools.partial(analysis_kernel, members),
         out_shape=(
@@ -293,8 +300,7 @@
         scratch_shapes=[
             pltpu.VMEM(prior_state_deviation.shape, jnp.float32),
             pltpu.VMEM(prior_state_deviation.shape, jnp.float32),
-            pltpu.VMEM((groups, members, LANES), jnp.float32),
-            pltpu.VMEM((LANES, LANES), jnp.float32),
+            pltpu.VMEM((SUB, LANES), jnp.float32),
             pltpu.VMEM((LANES, LANES), jnp.float32),
             pltpu.VMEM((groups, LANES, 2 * LANES), jnp.bfloat16),
             pltpu.SemaphoreType.DMA((groups,)),

time: 78.2 us -> 70.2 us (0.90)
  Pallas kernels: 22.1 us -> 17.4 us
  blocking collectives: 53.9 us -> 51 us
    all_to_all x2, blocking collectives: 53.9 us -> 46.3 us  [the longest x1 24.1 us: local(): lax.all_to_all(packed.reshape(parts, share), CORE_FIRST, 0, 0, tiled=True)]
    all_gather x0 -> x1, blocking collectives: none -> 4.71 us  [local(): gathered = lax.all_gather(own_half, CORE, axis=0, tiled=False)]
    pallas_call x1, Pallas kernels: 19.9 us -> 15.2 us  [local(): pl.pallas_call(functools.partial(analysis_kernel, members), out_shape=(ja...]
where the time goes in v2:
time: 70.2 us; the launch traced here: 70 us
  blocking collectives  51 us (73%)
  Pallas kernels  17.4 us (25%)
  between operations  1.29 us (2%)
    all_to_all x1, blocking collectives, local(): lax.all_to_all(packed.reshape(parts, share), CORE_FIRST, 0, 0, tiled=True)  24.1 us
    all_to_all x1, blocking collectives, local(): own_half = lax.all_to_all(copies, SAME_CORE, 0, 0, tiled=True)  22.2 us
    pallas_call x1, Pallas kernels, local(): pl.pallas_call(functools.partial(analysis_kernel, members), out_shape=(ja...  15.2 us
    all_gather x1, blocking collectives, local(): gathered = lax.all_gather(own_half, CORE, axis=0, tiled=False)  4.71 us
    pallas_call x1, Pallas kernels, local(): pl.pallas_call(functools.partial(statistics_kernel, members), out_shape=j...  2.18 us

profile of v2, /device:TPU:1, one launch (start us, length us, event | category | flops | bytes accessed | tf_op | source)
XLA Modules:
  0.0 70.0 jit_solution(5455633089893700006)
XLA Ops:
  1.3 2.2 %shard_map.95 = f32[320,128]{1,0:T(8,128)} custom-call(s32[1]{0:T(128)} %bitcast.band_ref, s32[4]{0:T(128)} %tile_block_ref.1, s32[1]{0:T(128)S(6)} %copy.11.obs_count_ref, s32[4,4]{1,0:T(4,128)} %block_mask_ref.3, f32[80,512]{1,0:T(8,128)} %priors_ref.1, f32[1,512]{1,0:T(1,128)} %bitcast.7, f32[1,512]{1,0:T(1,128)} %bitcast.8), custom_call_target="tpu_custom_call" | custom-call | tf_op jit(solution)/shard_map/pallas_call | solution.py:271
  3.5 24.1 %all_to_all.15 = f32[64,1,640]{2,1,0:T(1,128)S(1)} all-to-all(f32[64,1,640]{2,1,0:T(1,128)} %bitcast.6), channel_id=1, replica_groups=mesh['band'=4,'col_0'=8,'col_1'=4,'col_2'=2] {'col_2','col_0','col_1'}, dimensions={0} | all-to-all | bytes 327680 | tf_op jit(solution)/shard_map/all_to_all | solution.py:286
  27.6 0.1 reduce_sum.9
  27.7 0.2 broadcast_in_dim.2
  27.9 22.2 %all_to_all.16 = f32[128,1,640]{2,1,0:T(1,128)S(1)} all-to-all(f32[128,1,640]{2,1,0:T(1,128)S(1)} %broadcast_in_dim.2), channel_id=1, replica_groups=mesh['band'=4,'col_0'=8,'col_1'=4,'col_2'=2] {'band','col_0','col_1'}, dimensions={0} | all-to-all | bytes 655360 | tf_op jit(solution)/shard_map/all_to_all | solution.py:289
  50.0 4.7 %all_gather.3.gathered_ref = f32[2,640,128]{2,1,0:T(8,128)} all-gather(f32[1,640,128]{2,1,0:T(8,128)S(1)} %bitcast.5), channel_id=1, replica_groups=mesh['band'=4,'col_0'=8,'col_1'=4,'col_2'=2] {'col_2'}, dimensions={0}, use_global_device_ids=true | all-gather | bytes 983040 | tf_op jit(solution)/shard_map/all_gather | solution.py:291
  54.8 15.2 %shard_map.96 = (f32[4,16,256]{2,1,0:T(8,128)}, f32[4,16,80,256]{3,2,1,0:T(8,128)}) custom-call(s32[4,4]{1,0:T(4,128)} %block_mask_ref.3, f32[2,640,128]{2,1,0:T(8,128)} %all_gather.3.gathered_ref, f32[4,16,256]{2,1,0:T(8,128)} %mean_ref.1, f32[4,16,80,256]{3,2,1,0:T(8,128)} %deviation_hbm.1), custom_call_target="tpu_custom_call" | custom-call | tf_op jit(solution)/shard_map/pallas_call | solution.py:292

commit v3 on v2

--- a/solution.py
+++ b/solution.py
@@ -16,6 +16,7 @@
 HIGHEST = lax.Precision.HIGHEST
 LANES = 128
 SUB = 8
+START = 83
 
 
 def lane_of(shape):
@@ -46,7 +47,7 @@
     tiles = tile_block_ref.shape[0]
     tile_rows = priors_ref.shape[1] // tiles
     bands = block_mask_ref.shape[0]
-    pairs = 1 << (bands - 2)
+    histories = 1 << (bands - 1)
     band = band_ref[0]
     count = obs_count_ref[0]
     lane = lane_of((members, LANES))
@@ -81,22 +82,43 @@
             total = total + moments[t] * jnp.where(history[t] == s, 1.0, 0.0)
         return total
 
-    for p in range(pairs):
-        even = of_history(2 * p)
-        odd = of_history(2 * p + 1)
+    half = members // 2
+    top = row_of((half, LANES))
+    spot = lane_of((half, LANES))
+    for q in range(-(-histories // 3)):
+        even = of_history(3 * q)
+        odd = of_history(3 * q + 1)
         packed = jnp.where(lane > row, pltpu.roll(odd, 1, 1), even)
         packed = jnp.where(lane == members + 2, pltpu.roll(even, 2, 1), packed)
-        packed = jnp.where(lane > members + 2, 0.0, packed)
-        out_ref[pl.ds(p * members, members), :] = packed
-
-
-def unpack(packed, scratch, members):
+        if 3 * q + 2 < histories:
+            third = of_history(3 * q + 2)
+            left = pltpu.roll(third, START, 1)
+            right = pltpu.roll(third, START + 1 - half, 1)
+            upper = jnp.where(spot - START <= top, left[:half], right[half:])
+            lower = left[half:]
+            below = jnp.concatenate([upper, lower], axis=0)
+            below = jnp.where(lane == START + half + 1, right, below)
+            below = jnp.where(lane > START + half + 1, 0.0, below)
+            packed = jnp.where(lane > members + 2, below, packed)
+        else:
+            packed = jnp.where(lane > members + 2, 0.0, packed)
+        out_ref[pl.ds(q * members, members), :] = packed
+    used = -(-histories // 3) * members
+    if used < out_ref.shape[0]:
+        rest = out_ref.shape[0] - used
+        out_ref[pl.ds(used, rest), :] = jnp.zeros((rest, LANES), jnp.float32)
+
+
+def flipped(value, scratch, members):
+    scratch[...] = jnp.concatenate(
+        [value, jnp.zeros((LANES - members, LANES), jnp.float32)], axis=0
+    ).T
+
+
+def unpack_two(packed, scratch, members):
     lane = lane_of((members, LANES))
     row = row_of((members, LANES))
-    square = jnp.concatenate(
-        [packed, jnp.zeros((LANES - members, LANES), jnp.float32)], axis=0
-    )
-    scratch[...] = square.T
+    flipped(packed, scratch, members)
     even = jnp.where(lane <= row, packed, scratch[pl.ds(0, members), :])
     even = jnp.where(lane == members, pltpu.roll(packed, LANES - 2, 1), even)
     even = jnp.where(lane > members, 0.0, even)
@@ -105,11 +127,29 @@
     return even, odd
 
 
-def inverse_and_solution(system, nothing, members):
+def unpack_third(packed, scratch, members):
+    half = members // 2
+    lane = lane_of((members, LANES))
+    row = row_of((members, LANES))
+    left = pltpu.roll(packed, LANES - START, 1)
+    right = pltpu.roll(packed, LANES - (START + 1 - half), 1)
+    corner = jnp.concatenate([right[:half], right[:half]], axis=0)
+    once = jnp.where(lane < half, left, corner)
+    flipped(jnp.where(lane < members, once, 0.0), scratch, members)
+    held = ((lane < half) & ((row >= half) | (lane <= row))) | (
+        (lane >= half) & (row >= half) & (lane >= row)
+    )
+    third = jnp.where(held, once, scratch[pl.ds(0, members), :])
+    third = jnp.where(lane == members, right, third)
+    return jnp.where(lane > members, 0.0, third)
+
+
+def inverse_and_solution(system, nothing, members, tasks):
     blocks = members // SUB
     rows = [system[SUB * i : SUB * (i + 1), :] for i in range(blocks)]
     lane = lane_of((SUB, LANES))
     sub = row_of((SUB, LANES))
+    issued = 0
     for k in range(blocks):
         base = SUB * k
         inside = (lane >= base) & (lane < base + SUB)
@@ -128,6 +168,9 @@
             for j in range(i + 1, SUB):
                 other = jnp.broadcast_to(spread[j][i : i + 1, :], (SUB, LANES)) * scale
                 spread[j] = jnp.where(here, other, spread[j] - factor * other)
+        while issued < len(tasks) * (k + 1) // blocks:
+            tasks[issued]()
+            issued += 1
         fresh = [jnp.broadcast_to(pivot[i : i + 1, :], (SUB, LANES)) for i in range(SUB)]
         order = [(k + 1 + m) % blocks for m in range(blocks - 1)]
         for m in order:
@@ -143,7 +186,9 @@
 def analysis_kernel(
     members,
     block_mask_ref,
-    gathered_ref,
+    core_ref,
+    mine_ref,
+    other_ref,
     mean_ref,
     deviation_hbm,
     mean_out_ref,
@@ -151,7 +196,10 @@
     deviation,
     perturb,
     nothing,
-    flip,
+    flips,
+    moments,
+    maps,
+    transforms,
     lhs,
     in_sem,
     out_sem,
@@ -159,10 +207,9 @@
     bands, groups = block_mask_ref.shape
     levels = mean_ref.shape[1]
     columns = mean_ref.shape[2]
-    cores = gathered_ref.shape[0]
-    pairs = 1 << (bands - 2)
     lane = lane_of((members, LANES))
     row = row_of((members, LANES))
+    diagonal = lane == row
     loads = [
         pltpu.make_async_copy(deviation_hbm.at[g], deviation.at[g], in_sem.at[g])
         for g in range(groups)
@@ -170,61 +217,110 @@
     for load in loads:
         load.start()
     nothing[...] = jnp.zeros_like(nothing)
-
-    by_band = []
-    for b in range(bands):
-        found = []
-        for p in range(max(1, (1 << b) // 2)):
-            half = pairs // cores
-            at = (b * half + p % half) * members
-            packed = gathered_ref[p // half, pl.ds(at, members), :]
-            even, odd = unpack(packed, flip, members)
-            found.append(even)
-            if b > 0:
-                found.append(odd)
-        by_band.append(found)
-
-    diagonal = lane == row
-    current = [jnp.where(diagonal, 1.0, 0.0) for _ in range(groups)]
     lower = jnp.where(
         (row_of((LANES - members, LANES)) == 0) & (lane_of((LANES - members, LANES)) == members),
         1.0,
         0.0,
     )
     for b in range(bands):
-        moment = by_band[b][0]
+        transforms[b, pl.ds(members, LANES - members), :] = lower
+    band_rows = mine_ref.shape[0] // bands
+    first_core = core_ref[0] == 0
+
+    def tile(b, q):
+        pieces = []
+        for core in range(2):
+            low = max(q * members, core * band_rows)
+            high = min((q + 1) * members, (core + 1) * band_rows)
+            if low < high:
+                at = pl.ds(b * band_rows + low - core * band_rows, high - low)
+                mine, other = mine_ref[at, :], other_ref[at, :]
+                own = first_core if core == 0 else jnp.logical_not(first_core)
+                pieces.append(jnp.where(own, mine, other))
+        return pieces[0] if len(pieces) == 1 else jnp.concatenate(pieces, axis=0)
+
+    used = [0]
+
+    def scratch():
+        used[0] += 1
+        return flips.at[used[0] % flips.shape[0]]
+
+    def slot(b, s):
+        return (1 << b) - 1 + s
+
+    def unpack_first(b, q):
+        def task():
+            even, odd = unpack_two(tile(b, q), scratch(), members)
+            moments[slot(b, 3 * q)] = even
+            if 3 * q + 1 < (1 << b):
+                moments[slot(b, 3 * q + 1)] = odd
+
+        return task
+
+    def unpack_last(b, q):
+        def task():
+            moments[slot(b, 3 * q + 2)] = unpack_third(tile(b, q), scratch(), members)
+
+        return task
+
+    def merge(stage, b, s):
+        def task():
+            moved = matmul(moments[slot(b, 2 * s + 1)], transforms[stage])
+            square = transforms[stage, pl.ds(0, members), pl.ds(0, members)]
+            moments[slot(b, s)] = moments[slot(b, 2 * s)] + matmul(square, moved)
+
+        return task
+
+    def update(stage, g):
+        def task():
+            new = transforms[stage, pl.ds(0, members), :]
+            if stage == 0:
+                old = jnp.where(diagonal, 1.0, 0.0)
+            else:
+                old = maps[g]
+                new = matmul(old, transforms[stage])
+            maps[g] = jnp.where(block_mask_ref[stage, g] > 0, new, old)
+
+        return task
+
+    unpack_first(0, 0)()
+    during = [[] for _ in range(bands)]
+    for b in range(1, bands):
+        for q in range(-(-(1 << b) // 3)):
+            during[0].append(unpack_first(b, q))
+            if 3 * q + 2 < (1 << b):
+                during[0].append(unpack_last(b, q))
+    for stage in range(bands - 1):
+        for later in range(stage + 2, bands):
+            for s in range(1 << (later - stage - 1)):
+                during[stage + 1].append(merge(stage, later, s))
+        for g in range(groups):
+            during[stage + 1].append(update(stage, g))
+
+    for b in range(bands):
+        moment = moments[slot(b, 0)]
         system = jnp.where(
             lane == members, -moment, moment + jnp.where(diagonal, members - 1.0, 0.0)
         )
-        solved = inverse_and_solution(system, nothing[...], members)
-        transform = jnp.where(
+        solved = inverse_and_solution(system, nothing[...], members, during[b])
+        transforms[b, pl.ds(0, members), :] = jnp.where(
             lane < members,
             jnp.where(diagonal, 0.5, 0.0) + (0.5 * (members - 1)) * solved,
             jnp.where(lane == members, solved, 0.0),
         )
-        augmented = jnp.concatenate([transform, lower], axis=0)
-        for later in range(b + 1, bands):
-            held = by_band[later]
-            merged = []
-            for s in range(0, len(held), 2):
-                moved = matmul(held[s + 1], augmented)
-                moved = matmul(transform, moved, ((0,), (0,)))[:members, :]
-                merged.append(held[s] + moved)
-            by_band[later] = merged
-        for g in range(groups):
-            moved = transform if b == 0 else matmul(current[g], augmented)
-            current[g] = jnp.where(block_mask_ref[b, g] > 0, moved, current[g])
-
+        if b + 1 < bands:
+            merge(b, b + 1, 0)()
+
+    stores = []
+    zero = jnp.zeros((2 * LANES - 3 * members, columns), jnp.bfloat16)
     for g in range(groups):
-        high = current[g].astype(jnp.bfloat16).astype(jnp.float32)
-        low = (current[g] - high).astype(jnp.bfloat16).astype(jnp.float32)
+        update(bands - 1, g)()
+        high = maps[g].astype(jnp.bfloat16).astype(jnp.float32)
+        low = (maps[g] - high).astype(jnp.bfloat16).astype(jnp.float32)
         stack = jnp.concatenate(
             [high, low, high, jnp.zeros((2 * LANES - 3 * members, LANES), jnp.float32)], axis=0
         )
         lhs[g] = stack.T.astype(jnp.bfloat16)
-
-    stores = []
-    zero = jnp.zeros((2 * LANES - 3 * members, columns), jnp.bfloat16)
     for g in range(groups):
         loads[g].wait()
 
@@ -261,18 +357,21 @@
     members = obs_priors.shape[0]
     groups, levels, columns = prior_state_mean.shape
     bands = block_mask.shape[0]
-    pairs = 1 << (bands - 2)
+    histories = 1 << (bands - 1)
     parts = lax.axis_size(COL)
     everyone = lax.axis_size(SAME_CORE)
+    band_rows = -(-(-(-histories // 3) * members) // parts) * parts
+    share = band_rows * LANES // parts
     vmem = pl.BlockSpec(memory_space=pltpu.VMEM)
     smem = pl.BlockSpec(memory_space=pltpu.SMEM)
     hbm = pl.BlockSpec(memory_space=pl.ANY)
     my_band = lax.axis_index("band").astype(jnp.int32).reshape(1)
     packed = pl.pallas_call(
         functools.partial(statistics_kernel, members),
-        out_shape=jax.ShapeDtypeStruct((pairs * members, LANES), jnp.float32),
+        out_shape=jax.ShapeDtypeStruct((band_rows, LANES), jnp.float32),
         in_specs=[smem] * 4 + [vmem] * 3,
         out_specs=vmem,
+        compiler_params=pltpu.CompilerParams(vmem_limit_bytes=8 << 20),
     )(
         my_band,
         tile_block,
@@ -282,31 +381,34 @@
         innovation.reshape(1, -1),
         obs_precision.reshape(1, -1),
     )
-    share = pairs * members * LANES // parts
     received = lax.all_to_all(packed.reshape(parts, share), CORE_FIRST, 0, 0, tiled=True)
     summed = jnp.sum(received, axis=0, keepdims=True)
     copies = jnp.broadcast_to(summed, (everyone, share))
-    own_half = lax.all_to_all(copies, SAME_CORE, 0, 0, tiled=True)
-    own_half = own_half.reshape(-1, LANES)
-    gathered = lax.all_gather(own_half, CORE, axis=0, tiled=False)
+    mine = lax.all_to_all(copies, SAME_CORE, 0, 0, tiled=True).reshape(-1, LANES)
+    other = lax.ppermute(mine, CORE, [(0, 1), (1, 0)])
+    my_core = lax.axis_index(CORE).astype(jnp.int32).reshape(1)
     return pl.pallas_call(
         functools.partial(analysis_kernel, members),
         out_shape=(
             jax.ShapeDtypeStruct(prior_state_mean.shape, jnp.float32),
             jax.ShapeDtypeStruct(prior_state_deviation.shape, jnp.float32),
         ),
-        in_specs=[smem, vmem, vmem, hbm],
+        in_specs=[smem, smem, vmem, vmem, vmem, hbm],
         out_specs=(vmem, hbm),
         scratch_shapes=[
             pltpu.VMEM(prior_state_deviation.shape, jnp.float32),
             pltpu.VMEM(prior_state_deviation.shape, jnp.float32),
             pltpu.VMEM((SUB, LANES), jnp.float32),
-            pltpu.VMEM((LANES, LANES), jnp.float32),
+            pltpu.VMEM((4, LANES, LANES), jnp.float32),
+            pltpu.VMEM(((1 << bands) - 1, members, LANES), jnp.float32),
+            pltpu.VMEM((groups, members, LANES), jnp.float32),
+            pltpu.VMEM((bands, LANES, LANES), jnp.float32),
             pltpu.VMEM((groups, LANES, 2 * LANES), jnp.bfloat16),
             pltpu.SemaphoreType.DMA((groups,)),
             pltpu.SemaphoreType.DMA((groups,)),
         ],
-    )(block_mask, gathered, prior_state_mean, prior_state_deviation)
+        compiler_params=pltpu.CompilerParams(vmem_limit_bytes=50 << 20),
+    )(block_mask, my_core, mine, other, prior_state_mean, prior_state_deviation)
 
 
 def solution(mesh):

time: 70.2 us -> 71.1 us (1.013)
  blocking collectives: 51 us -> 44.3 us
  local copies, waits for them, and re-layouts: 0.17 us -> 5.27 us
  starting transfers between devices: 0 us -> 2.5 us
  Pallas kernels: 17.4 us -> 16 us
  waiting for transfers between devices: 0 us -> 1.16 us
    unnamed x0 -> x14, local copies, waits for them, and re-layouts: none -> 5.13 us
    all_gather x1 -> x0, blocking collectives: 4.71 us -> none  [local(): gathered = lax.all_gather(own_half, CORE, axis=0, tiled=False)]
    ppermute x0 -> x1, starting transfers between devices: none -> 2.5 us  [local(): other = lax.ppermute(mine, CORE, [(0, 1), (1, 0)])]
    all_to_all x1, blocking collectives: 22.2 us -> 20.7 us  [local(): lax.all_to_all(copies, SAME_CORE, 0, 0, tiled=True).reshape(-1, LANES)]
    ppermute x0 -> x1, waiting for transfers between devices: none -> 1.16 us  [local(): other = lax.ppermute(mine, CORE, [(0, 1), (1, 0)])]
    pallas_call x1, Pallas kernels: 2.18 us -> 1.17 us  [local(): pl.pallas_call(functools.partial(statistics_kernel, members), out_shape=j...]
  transfers between devices with their start and end apart: 0 -> 1, of which waited for: 0 -> 1; matrix products, arithmetic and copies ran while one was open for 0% -> 0% of each run, Pallas kernels for 0% -> 0%
where the time goes in v3:
time: 71.1 us; the launch traced here: 70.8 us
  blocking collectives  44.3 us (62%)
  Pallas kernels  16 us (23%)
  local copies, waits for them, and re-layouts  5.27 us (7%)
  starting transfers between devices  2.5 us (4%)
  between operations  1.47 us (2%)
  waiting for transfers between devices  1.16 us (2%)
    all_to_all x1, blocking collectives, local(): lax.all_to_all(packed.reshape(parts, share), CORE_FIRST, 0, 0, tiled=True)  23.5 us
    all_to_all x1, blocking collectives, local(): lax.all_to_all(copies, SAME_CORE, 0, 0, tiled=True).reshape(-1, LANES)  20.7 us
    pallas_call x1, Pallas kernels, local(): pl.pallas_call(functools.partial(analysis_kernel, members), out_shape=(ja...  14.9 us
    unnamed x14, local copies, waits for them, and re-layouts  5.13 us
    ppermute x1, starting transfers between devices, local(): other = lax.ppermute(mine, CORE, [(0, 1), (1, 0)])  2.5 us
  transfers between devices with their start and end apart: 1, of which 1 were waited for; matrix products, arithmetic and copies ran while one was open for 0% of the time, Pallas kernels for 0%

profile of v3, /device:TPU:1, one launch (start us, length us, event | category | flops | bytes accessed | tf_op | source)
XLA Modules:
  0.0 70.8 jit_solution(14371592917556212556)
XLA Ops:
  1.3 0.0 copy-start
  1.3 0.9 %copy-done = f32[80,512]{1,0:T(8,128)S(1)} copy-done((f32[80,512]{1,0:T(8,128)S(1)}, f32[80,512]{1,0:T(8,128)}, u32[]{:S(2)}) %copy-start) | copy-done | bytes 163864
  2.2 0.0 copy-start.2
  2.2 0.7 copy-done.2
  2.9 0.0 copy-start.4
  2.9 0.7 copy-done.4
  3.6 0.0 copy-start.5
  3.6 0.7 copy-done.5
  4.2 0.0 copy-start.6
  4.2 0.7 copy-done.6
  4.9 1.2 %shard_map.95 = f32[256,128]{1,0:T(8,128)S(1)} custom-call(s32[1]{0:T(128)} %bitcast.1.band_ref, s32[4]{0:T(128)S(1)} %copy-done.6, s32[1]{0:T(128)S(6)} %copy.11.obs_count_ref, s32[4,4]{1,0:T(4,128)S(1)} %copy-done.2, f32[80,512]{1,0:T(8,128)S(1)} %copy-done, f32[1,512]{1,0:T(1,128)S(1)} %bitcast.9, f32[1,512]{1,0:T(1,128)S(1)} %bitcast.10), custom_call_target="tpu_custom_call" | custom-call | tf_op jit(solution)/shard_map/pallas_call | solution.py:369
  6.1 23.5 %all_to_all.15 = f32[64,1,512]{2,1,0:T(1,128)S(1)} all-to-all(f32[64,1,512]{2,1,0:T(1,128)S(1)} %bitcast.8), channel_id=1, replica_groups=mesh['band'=4,'col_0'=8,'col_1'=4,'col_2'=2] {'col_2','col_0','col_1'}, dimensions={0} | all-to-all | bytes 262144 | tf_op jit(solution)/shard_map/all_to_all | solution.py:384
  29.6 0.1 reduce_sum.9
  29.7 0.1 broadcast_in_dim.2
  29.8 20.7 %all_to_all.16 = f32[128,1,512]{2,1,0:T(1,128)S(1)} all-to-all(f32[128,1,512]{2,1,0:T(1,128)S(1)} %broadcast_in_dim.2), channel_id=1, replica_groups=mesh['band'=4,'col_0'=8,'col_1'=4,'col_2'=2] {'band','col_0','col_1'}, dimensions={0} | all-to-all | bytes 524288 | tf_op jit(solution)/shard_map/all_to_all | solution.py:387
  50.6 2.5 %collective-permute-start = (f32[512,128]{1,0:T(8,128)S(1)}, f32[512,128]{1,0:T(8,128)S(1)}, u32[]{:S(2)}, u32[]{:S(2)}) collective-permute-start(f32[512,128]{1,0:T(8,128)S(1)} %bitcast.6), channel_id=1, source_target_pairs={{0,1},{1,0},{2,3},{3,2},{4,5},{5,4},{6,7},{7,6},{8,9},{9,8},{10,11... | collective-permute-start | bytes 786440 | tf_op jit(solution)/shard_map/ppermute | solution.py:388
  53.1 1.2 %collective-permute-done.other_ref = f32[512,128]{1,0:T(8,128)S(1)} collective-permute-done((f32[512,128]{1,0:T(8,128)S(1)}, f32[512,128]{1,0:T(8,128)S(1)}, u32[]{:S(2)}, u32[]{:S(2)}) %collective-permute-start) | collective-permute-done | bytes 262176 | tf_op jit(solution)/shard_map/ppermute | solution.py:388
  54.2 0.0 copy-start.1
  54.2 0.8 %copy-done.1 = f32[4,16,256]{2,1,0:T(8,128)S(1)} copy-done((f32[4,16,256]{2,1,0:T(8,128)S(1)}, f32[4,16,256]{2,1,0:T(8,128)}, u32[]{:S(2)}) %copy-start.1) | copy-done | bytes 65560
  55.1 0.0 copy-start.3
  55.1 0.7 copy-done.3
  55.8 14.9 %shard_map.96 = (f32[4,16,256]{2,1,0:T(8,128)}, f32[4,16,80,256]{3,2,1,0:T(8,128)}) custom-call(s32[4,4]{1,0:T(4,128)S(1)} %copy-done.3, s32[1]{0:T(128)} %bitcast.core_ref, f32[512,128]{1,0:T(8,128)S(1)} %bitcast.7, f32[512,128]{1,0:T(8,128)S(1)} %collective-permute-done.other_ref, f32[4,16,256]{2,1,0:T(8,128)S(1)} %copy-done.1, ...), custom_call_target="tpu_custom_call" | custom-call | tf_op jit(solution)/shard_map/pallas_call | solution.py:390
Async XLA Ops:
  1.3 0.9 %copy-start = (f32[80,512]{1,0:T(8,128)S(1)}, f32[80,512]{1,0:T(8,128)}, u32[]{:S(2)}) copy-start(f32[80,512]{1,0:T(8,128)} %priors_ref.1) | copy-start | bytes 491524
  2.2 0.7 copy-start.2
  2.9 0.7 copy-start.4
  3.6 0.7 copy-start.5
  4.2 0.7 copy-start.6
  50.6 3.7 %collective-permute-start = (f32[512,128]{1,0:T(8,128)S(1)}, f32[512,128]{1,0:T(8,128)S(1)}, u32[]{:S(2)}, u32[]{:S(2)}) collective-permute-start(f32[512,128]{1,0:T(8,128)S(1)} %bitcast.6), channel_id=1, source_target_pairs={{0,1},{1,0},{2,3},{3,2},{4,5},{5,4},{6,7},{7,6},{8,9},{9,8},{10,11... | collective-permute-start | bytes 786440 | tf_op jit(solution)/shard_map/ppermute | solution.py:388
  54.2 0.8 %copy-start.1 = (f32[4,16,256]{2,1,0:T(8,128)S(1)}, f32[4,16,256]{2,1,0:T(8,128)}, u32[]{:S(2)}) copy-start(f32[4,16,256]{2,1,0:T(8,128)} %mean_ref.1) | copy-start | bytes 196612
  55.1 0.7 copy-start.3

commit v4 on v3

--- a/solution.py
+++ b/solution.py
@@ -355,6 +355,7 @@
     prior_state_deviation,
 ):
     members = obs_priors.shape[0]
+    in_hbm = functools.partial(pltpu.with_memory_space_constraint, memory_space=pltpu.HBM)
     groups, levels, columns = prior_state_mean.shape
     bands = block_mask.shape[0]
     histories = 1 << (bands - 1)
@@ -374,12 +375,12 @@
         compiler_params=pltpu.CompilerParams(vmem_limit_bytes=8 << 20),
     )(
         my_band,
-        tile_block,
+        in_hbm(tile_block),
         obs_count,
-        block_mask,
-        obs_priors,
-        innovation.reshape(1, -1),
-        obs_precision.reshape(1, -1),
+        in_hbm(block_mask),
+        in_hbm(obs_priors),
+        in_hbm(innovation.reshape(1, -1)),
+        in_hbm(obs_precision.reshape(1, -1)),
     )
     received = lax.all_to_all(packed.reshape(parts, share), CORE_FIRST, 0, 0, tiled=True)
     summed = jnp.sum(received, axis=0, keepdims=True)
@@ -408,7 +409,7 @@
             pltpu.SemaphoreType.DMA((groups,)),
         ],
         compiler_params=pltpu.CompilerParams(vmem_limit_bytes=50 << 20),
-    )(block_mask, my_core, mine, other, prior_state_mean, prior_state_deviation)
+    )(in_hbm(block_mask), my_core, mine, other, in_hbm(prior_state_mean), in_hbm(prior_state_deviation))
 
 
 def solution(mesh):

time: 71.1 us -> 66.5 us (0.935)
  local copies, waits for them, and re-layouts: 5.27 us -> 0.14 us
    unnamed x14 -> x0, local copies, waits for them, and re-layouts: 5.13 us -> none
where the time goes in v4:
time: 66.5 us; the launch traced here: 66.3 us
  blocking collectives  44.3 us (67%)
  Pallas kernels  16.7 us (25%)
  starting transfers between devices  2.5 us (4%)
  between operations  1.45 us (2%)
  waiting for transfers between devices  1.16 us (2%)
    all_to_all x1, blocking collectives, local(): lax.all_to_all(packed.reshape(parts, share), CORE_FIRST, 0, 0, tiled=True)  23.5 us
    all_to_all x1, blocking collectives, local(): lax.all_to_all(copies, SAME_CORE, 0, 0, tiled=True).reshape(-1, LANES)  20.7 us
    pallas_call x1, Pallas kernels, local(): pl.pallas_call(functools.partial(analysis_kernel, members), out_shape=(ja...  15.2 us
    ppermute x1, starting transfers between devices, local(): other = lax.ppermute(mine, CORE, [(0, 1), (1, 0)])  2.5 us
    pallas_call x1, Pallas kernels, local(): pl.pallas_call(functools.partial(statistics_kernel, members), out_shape=j...  1.53 us
  transfers between devices with their start and end apart: 1, of which 1 were waited for; matrix products, arithmetic and copies ran while one was open for 0% of the time, Pallas kernels for 0%

profile of v4, /device:TPU:1, one launch (start us, length us, event | category | flops | bytes accessed | tf_op | source)
XLA Modules:
  0.0 66.3 jit_solution(7961493806582249696)
XLA Ops:
  1.3 1.5 %shard_map.95 = f32[256,128]{1,0:T(8,128)S(1)} custom-call(s32[1]{0:T(128)} %bitcast.1.band_ref, s32[4]{0:T(128)} %tile_block_ref.1, s32[1]{0:T(128)S(6)} %copy.11.obs_count_ref, s32[4,4]{1,0:T(4,128)} %block_mask_ref.3, f32[80,512]{1,0:T(8,128)} %priors_ref.1, f32[1,512]{1,0:T(1,128)} %bitcast.9, f32[1,512]{1,0:T(1,128)} %bitcast.10), custom_call_target="tpu_custom_call" | custom-call | tf_op jit(solution)/shard_map/pallas_call | solution.py:370
  2.8 23.5 %all_to_all.15 = f32[64,1,512]{2,1,0:T(1,128)S(1)} all-to-all(f32[64,1,512]{2,1,0:T(1,128)S(1)} %bitcast.8), channel_id=1, replica_groups=mesh['band'=4,'col_0'=8,'col_1'=4,'col_2'=2] {'col_2','col_0','col_1'}, dimensions={0} | all-to-all | bytes 262144 | tf_op jit(solution)/shard_map/all_to_all | solution.py:385
  26.4 0.1 reduce_sum.9
  26.5 0.1 broadcast_in_dim.2
  26.6 20.7 %all_to_all.16 = f32[128,1,512]{2,1,0:T(1,128)S(1)} all-to-all(f32[128,1,512]{2,1,0:T(1,128)S(1)} %broadcast_in_dim.2), channel_id=1, replica_groups=mesh['band'=4,'col_0'=8,'col_1'=4,'col_2'=2] {'band','col_0','col_1'}, dimensions={0} | all-to-all | bytes 524288 | tf_op jit(solution)/shard_map/all_to_all | solution.py:388
  47.3 2.5 %collective-permute-start = (f32[512,128]{1,0:T(8,128)S(1)}, f32[512,128]{1,0:T(8,128)S(1)}, u32[]{:S(2)}, u32[]{:S(2)}) collective-permute-start(f32[512,128]{1,0:T(8,128)S(1)} %bitcast.6), channel_id=1, source_target_pairs={{0,1},{1,0},{2,3},{3,2},{4,5},{5,4},{6,7},{7,6},{8,9},{9,8},{10,11... | collective-permute-start | bytes 786440 | tf_op jit(solution)/shard_map/ppermute | solution.py:389
  49.8 1.2 %collective-permute-done.other_ref = f32[512,128]{1,0:T(8,128)S(1)} collective-permute-done((f32[512,128]{1,0:T(8,128)S(1)}, f32[512,128]{1,0:T(8,128)S(1)}, u32[]{:S(2)}, u32[]{:S(2)}) %collective-permute-start) | collective-permute-done | bytes 262176 | tf_op jit(solution)/shard_map/ppermute | solution.py:389
  51.0 15.2 %shard_map.96 = (f32[4,16,256]{2,1,0:T(8,128)}, f32[4,16,80,256]{3,2,1,0:T(8,128)}) custom-call(s32[4,4]{1,0:T(4,128)} %block_mask_ref.3, s32[1]{0:T(128)} %bitcast.core_ref, f32[512,128]{1,0:T(8,128)S(1)} %bitcast.7, f32[512,128]{1,0:T(8,128)S(1)} %collective-permute-done.other_ref, f32[4,16,256]{2,1,0:T(8,128)} %mean_ref.1, f32[4,16,80,256]{3,2,1,0:T(8,128)} %deviation_hbm.1), custom_call_target="tpu_custom_call" | custom-call | tf_op jit(solution)/shard_map/pallas_call | solution.py:391
Async XLA Ops:
  47.3 3.7 %collective-permute-start = (f32[512,128]{1,0:T(8,128)S(1)}, f32[512,128]{1,0:T(8,128)S(1)}, u32[]{:S(2)}, u32[]{:S(2)}) collective-permute-start(f32[512,128]{1,0:T(8,128)S(1)} %bitcast.6), channel_id=1, source_target_pairs={{0,1},{1,0},{2,3},{3,2},{4,5},{5,4},{6,7},{7,6},{8,9},{9,8},{10,11... | collective-permute-start | bytes 786440 | tf_op jit(solution)/shard_map/ppermute | solution.py:389

commit v5 on v4

--- a/solution.py
+++ b/solution.py
@@ -144,6 +144,10 @@
     return jnp.where(lane > members, 0.0, third)
 
 
+def row_at(value, i):
+    return jnp.broadcast_to(value[i : i + 1, :], (SUB, LANES))
+
+
 def inverse_and_solution(system, nothing, members, tasks):
     blocks = members // SUB
     rows = [system[SUB * i : SUB * (i + 1), :] for i in range(blocks)]
@@ -159,19 +163,27 @@
             for j in range(SUB)
         ]
         pivot = jnp.where(inside, jnp.where(lane - base == sub, 1.0, 0.0), pivot)
-        for i in range(SUB):
-            here = sub == i
-            scale = 1.0 / jnp.broadcast_to(spread[i][i : i + 1, :], (SUB, LANES))
-            own = jnp.broadcast_to(pivot[i : i + 1, :], (SUB, LANES)) * scale
-            factor = spread[i]
-            pivot = jnp.where(here, own, pivot - factor * own)
-            for j in range(i + 1, SUB):
-                other = jnp.broadcast_to(spread[j][i : i + 1, :], (SUB, LANES)) * scale
-                spread[j] = jnp.where(here, other, spread[j] - factor * other)
+        for i in range(0, SUB, 2):
+            first, second = sub == i, sub == i + 1
+            one, two = spread[i], spread[i + 1]
+            a, b = row_at(one, i), row_at(two, i)
+            c, d = row_at(one, i + 1), row_at(two, i + 1)
+            scale = 1.0 / (a * d - b * c)
+
+            def eliminated(value):
+                top, low = row_at(value, i), row_at(value, i + 1)
+                own = (d * top - b * low) * scale
+                next_own = (a * low - c * top) * scale
+                rest = value - one * own - two * next_own
+                return jnp.where(first, own, jnp.where(second, next_own, rest))
+
+            for j in range(i + 2, SUB):
+                spread[j] = eliminated(spread[j])
+            pivot = eliminated(pivot)
         while issued < len(tasks) * (k + 1) // blocks:
             tasks[issued]()
             issued += 1
-        fresh = [jnp.broadcast_to(pivot[i : i + 1, :], (SUB, LANES)) for i in range(SUB)]
+        fresh = [row_at(pivot, i) for i in range(SUB)]
         order = [(k + 1 + m) % blocks for m in range(blocks - 1)]
         for m in order:
             held = rows[m]
@@ -271,15 +283,19 @@
 
         return task
 
-    def update(stage, g):
+    def update(stage):
         def task():
-            new = transforms[stage, pl.ds(0, members), :]
-            if stage == 0:
-                old = jnp.where(diagonal, 1.0, 0.0)
-            else:
-                old = maps[g]
-                new = matmul(old, transforms[stage])
-            maps[g] = jnp.where(block_mask_ref[stage, g] > 0, new, old)
+            if stage > 0:
+                moved = matmul(maps[...], transforms[stage])
+            for g in range(groups):
+                at = pl.ds(g * members, members)
+                if stage == 0:
+                    old = jnp.where(diagonal, 1.0, 0.0)
+                    new = transforms[stage, pl.ds(0, members), :]
+                else:
+                    old = maps[at, :]
+                    new = moved[g * members : (g + 1) * members, :]
+                maps[at, :] = jnp.where(block_mask_ref[stage, g] > 0, new, old)
 
         return task
 
@@ -294,8 +310,7 @@
         for later in range(stage + 2, bands):
             for s in range(1 << (later - stage - 1)):
                 during[stage + 1].append(merge(stage, later, s))
-        for g in range(groups):
-            during[stage + 1].append(update(stage, g))
+        during[stage + 1].append(update(stage))
 
     for b in range(bands):
         moment = moments[slot(b, 0)]
@@ -313,10 +328,11 @@
 
     stores = []
     zero = jnp.zeros((2 * LANES - 3 * members, columns), jnp.bfloat16)
+    update(bands - 1)()
     for g in range(groups):
-        update(bands - 1, g)()
-        high = maps[g].astype(jnp.bfloat16).astype(jnp.float32)
-        low = (maps[g] - high).astype(jnp.bfloat16).astype(jnp.float32)
+        final = maps[pl.ds(g * members, members), :]
+        high = final.astype(jnp.bfloat16).astype(jnp.float32)
+        low = (final - high).astype(jnp.bfloat16).astype(jnp.float32)
         stack = jnp.concatenate(
             [high, low, high, jnp.zeros((2 * LANES - 3 * members, LANES), jnp.float32)], axis=0
         )
@@ -402,7 +418,7 @@
             pltpu.VMEM((SUB, LANES), jnp.float32),
             pltpu.VMEM((4, LANES, LANES), jnp.float32),
             pltpu.VMEM(((1 << bands) - 1, members, LANES), jnp.float32),
-            pltpu.VMEM((groups, members, LANES), jnp.float32),
+            pltpu.VMEM((groups * members, LANES), jnp.float32),
             pltpu.VMEM((bands, LANES, LANES), jnp.float32),
             pltpu.VMEM((groups, LANES, 2 * LANES), jnp.bfloat16),
             pltpu.SemaphoreType.DMA((groups,)),

time: 66.5 us -> 66 us (level)
  no operation moved by 1% of the time
where the time goes in v5:
time: 66 us; the launch traced here: 65.7 us
  blocking collectives  44.3 us (67%)
  Pallas kernels  16.1 us (24%)
  starting transfers between devices  2.5 us (4%)
  between operations  1.45 us (2%)
  waiting for transfers between devices  1.16 us (2%)
    all_to_all x1, blocking collectives, local(): lax.all_to_all(packed.reshape(parts, share), CORE_FIRST, 0, 0, tiled=True)  23.5 us
    all_to_all x1, blocking collectives, local(): lax.all_to_all(copies, SAME_CORE, 0, 0, tiled=True).reshape(-1, LANES)  20.7 us
    pallas_call x1, Pallas kernels, local(): pl.pallas_call(functools.partial(analysis_kernel, members), out_shape=(ja...  14.6 us
    ppermute x1, starting transfers between devices, local(): other = lax.ppermute(mine, CORE, [(0, 1), (1, 0)])  2.5 us
    pallas_call x1, Pallas kernels, local(): pl.pallas_call(functools.partial(statistics_kernel, members), out_shape=j...  1.53 us
  transfers between devices with their start and end apart: 1, of which 1 were waited for; matrix products, arithmetic and copies ran while one was open for 0% of the time, Pallas kernels for 0%

profile of v5, /device:TPU:1, one launch (start us, length us, event | category | flops | bytes accessed | tf_op | source)
XLA Modules:
  0.0 65.7 jit_solution(6799944702909321235)
XLA Ops:
  1.3 1.5 %shard_map.95 = f32[256,128]{1,0:T(8,128)S(1)} custom-call(s32[1]{0:T(128)} %bitcast.1.band_ref, s32[4]{0:T(128)} %tile_block_ref.1, s32[1]{0:T(128)S(6)} %copy.11.obs_count_ref, s32[4,4]{1,0:T(4,128)} %block_mask_ref.3, f32[80,512]{1,0:T(8,128)} %priors_ref.1, f32[1,512]{1,0:T(1,128)} %bitcast.9, f32[1,512]{1,0:T(1,128)} %bitcast.10), custom_call_target="tpu_custom_call" | custom-call | tf_op jit(solution)/shard_map/pallas_call | solution.py:386
  2.8 23.5 %all_to_all.15 = f32[64,1,512]{2,1,0:T(1,128)S(1)} all-to-all(f32[64,1,512]{2,1,0:T(1,128)S(1)} %bitcast.8), channel_id=1, replica_groups=mesh['band'=4,'col_0'=8,'col_1'=4,'col_2'=2] {'col_2','col_0','col_1'}, dimensions={0} | all-to-all | bytes 262144 | tf_op jit(solution)/shard_map/all_to_all | solution.py:401
  26.4 0.1 reduce_sum.9
  26.5 0.1 broadcast_in_dim.2
  26.6 20.7 %all_to_all.16 = f32[128,1,512]{2,1,0:T(1,128)S(1)} all-to-all(f32[128,1,512]{2,1,0:T(1,128)S(1)} %broadcast_in_dim.2), channel_id=1, replica_groups=mesh['band'=4,'col_0'=8,'col_1'=4,'col_2'=2] {'band','col_0','col_1'}, dimensions={0} | all-to-all | bytes 524288 | tf_op jit(solution)/shard_map/all_to_all | solution.py:404
  47.3 2.5 %collective-permute-start = (f32[512,128]{1,0:T(8,128)S(1)}, f32[512,128]{1,0:T(8,128)S(1)}, u32[]{:S(2)}, u32[]{:S(2)}) collective-permute-start(f32[512,128]{1,0:T(8,128)S(1)} %bitcast.6), channel_id=1, source_target_pairs={{0,1},{1,0},{2,3},{3,2},{4,5},{5,4},{6,7},{7,6},{8,9},{9,8},{10,11... | collective-permute-start | bytes 786440 | tf_op jit(solution)/shard_map/ppermute | solution.py:405
  49.8 1.2 %collective-permute-done.other_ref = f32[512,128]{1,0:T(8,128)S(1)} collective-permute-done((f32[512,128]{1,0:T(8,128)S(1)}, f32[512,128]{1,0:T(8,128)S(1)}, u32[]{:S(2)}, u32[]{:S(2)}) %collective-permute-start) | collective-permute-done | bytes 262176 | tf_op jit(solution)/shard_map/ppermute | solution.py:405
  51.0 14.6 %shard_map.96 = (f32[4,16,256]{2,1,0:T(8,128)}, f32[4,16,80,256]{3,2,1,0:T(8,128)}) custom-call(s32[4,4]{1,0:T(4,128)} %block_mask_ref.3, s32[1]{0:T(128)} %bitcast.core_ref, f32[512,128]{1,0:T(8,128)S(1)} %bitcast.7, f32[512,128]{1,0:T(8,128)S(1)} %collective-permute-done.other_ref, f32[4,16,256]{2,1,0:T(8,128)} %mean_ref.1, f32[4,16,80,256]{3,2,1,0:T(8,128)} %deviation_hbm.1), custom_call_target="tpu_custom_call" | custom-call | tf_op jit(solution)/shard_map/pallas_call | solution.py:407
Async XLA Ops:
  47.3 3.7 %collective-permute-start = (f32[512,128]{1,0:T(8,128)S(1)}, f32[512,128]{1,0:T(8,128)S(1)}, u32[]{:S(2)}, u32[]{:S(2)}) collective-permute-start(f32[512,128]{1,0:T(8,128)S(1)} %bitcast.6), channel_id=1, source_target_pairs={{0,1},{1,0},{2,3},{3,2},{4,5},{5,4},{6,7},{7,6},{8,9},{9,8},{10,11... | collective-permute-start | bytes 786440 | tf_op jit(solution)/shard_map/ppermute | solution.py:405

commit v6 on v5

--- a/solution.py
+++ b/solution.py
@@ -169,12 +169,13 @@
             a, b = row_at(one, i), row_at(two, i)
             c, d = row_at(one, i + 1), row_at(two, i + 1)
             scale = 1.0 / (a * d - b * c)
+            a, b, c, d = a * scale, b * scale, c * scale, d * scale
 
             def eliminated(value):
                 top, low = row_at(value, i), row_at(value, i + 1)
-                own = (d * top - b * low) * scale
-                next_own = (a * low - c * top) * scale
-                rest = value - one * own - two * next_own
+                own = d * top - b * low
+                next_own = a * low - c * top
+                rest = value - (one * own + two * next_own)
                 return jnp.where(first, own, jnp.where(second, next_own, rest))
 
             for j in range(i + 2, SUB):
@@ -187,10 +188,10 @@
         order = [(k + 1 + m) % blocks for m in range(blocks - 1)]
         for m in order:
             held = rows[m]
-            total = jnp.where(inside, 0.0, held)
-            for i in range(SUB):
-                total = total - held[:, base + i : base + i + 1] * fresh[i]
-            rows[m] = total
+            terms = [held[:, base + i : base + i + 1] * fresh[i] for i in range(SUB)]
+            while len(terms) > 1:
+                terms = [terms[i] + terms[i + 1] for i in range(0, len(terms), 2)]
+            rows[m] = jnp.where(inside, 0.0, held) - terms[0]
         rows[k] = pivot
     return jnp.concatenate(rows, axis=0)
 

time: 66 us -> 66.3 us (level)
  no operation moved by 1% of the time
where the time goes in v6:
time: 66.3 us; the launch traced here: 66 us
  blocking collectives  44.3 us (67%)
  Pallas kernels  16.4 us (25%)
  starting transfers between devices  2.5 us (4%)
  between operations  1.45 us (2%)
  waiting for transfers between devices  1.16 us (2%)
    all_to_all x1, blocking collectives, local(): lax.all_to_all(packed.reshape(parts, share), CORE_FIRST, 0, 0, tiled=True)  23.5 us
    all_to_all x1, blocking collectives, local(): lax.all_to_all(copies, SAME_CORE, 0, 0, tiled=True).reshape(-1, LANES)  20.7 us
    pallas_call x1, Pallas kernels, local(): pl.pallas_call(functools.partial(analysis_kernel, members), out_shape=(ja...  14.9 us
    ppermute x1, starting transfers between devices, local(): other = lax.ppermute(mine, CORE, [(0, 1), (1, 0)])  2.5 us
    pallas_call x1, Pallas kernels, local(): pl.pallas_call(functools.partial(statistics_kernel, members), out_shape=j...  1.53 us
  transfers between devices with their start and end apart: 1, of which 1 were waited for; matrix products, arithmetic and copies ran while one was open for 0% of the time, Pallas kernels for 0%

profile of v6, /device:TPU:1, one launch (start us, length us, event | category | flops | bytes accessed | tf_op | source)
XLA Modules:
  0.0 66.0 jit_solution(1272503233714531989)
XLA Ops:
  1.3 1.5 %shard_map.95 = f32[256,128]{1,0:T(8,128)S(1)} custom-call(s32[1]{0:T(128)} %bitcast.1.band_ref, s32[4]{0:T(128)} %tile_block_ref.1, s32[1]{0:T(128)S(6)} %copy.11.obs_count_ref, s32[4,4]{1,0:T(4,128)} %block_mask_ref.3, f32[80,512]{1,0:T(8,128)} %priors_ref.1, f32[1,512]{1,0:T(1,128)} %bitcast.9, f32[1,512]{1,0:T(1,128)} %bitcast.10), custom_call_target="tpu_custom_call" | custom-call | tf_op jit(solution)/shard_map/pallas_call | solution.py:387
  2.8 23.5 %all_to_all.15 = f32[64,1,512]{2,1,0:T(1,128)S(1)} all-to-all(f32[64,1,512]{2,1,0:T(1,128)S(1)} %bitcast.8), channel_id=1, replica_groups=mesh['band'=4,'col_0'=8,'col_1'=4,'col_2'=2] {'col_2','col_0','col_1'}, dimensions={0} | all-to-all | bytes 262144 | tf_op jit(solution)/shard_map/all_to_all | solution.py:402
  26.4 0.1 reduce_sum.9
  26.5 0.1 broadcast_in_dim.2
  26.6 20.7 %all_to_all.16 = f32[128,1,512]{2,1,0:T(1,128)S(1)} all-to-all(f32[128,1,512]{2,1,0:T(1,128)S(1)} %broadcast_in_dim.2), channel_id=1, replica_groups=mesh['band'=4,'col_0'=8,'col_1'=4,'col_2'=2] {'band','col_0','col_1'}, dimensions={0} | all-to-all | bytes 524288 | tf_op jit(solution)/shard_map/all_to_all | solution.py:405
  47.3 2.5 %collective-permute-start = (f32[512,128]{1,0:T(8,128)S(1)}, f32[512,128]{1,0:T(8,128)S(1)}, u32[]{:S(2)}, u32[]{:S(2)}) collective-permute-start(f32[512,128]{1,0:T(8,128)S(1)} %bitcast.6), channel_id=1, source_target_pairs={{0,1},{1,0},{2,3},{3,2},{4,5},{5,4},{6,7},{7,6},{8,9},{9,8},{10,11... | collective-permute-start | bytes 786440 | tf_op jit(solution)/shard_map/ppermute | solution.py:406
  49.8 1.2 %collective-permute-done.other_ref = f32[512,128]{1,0:T(8,128)S(1)} collective-permute-done((f32[512,128]{1,0:T(8,128)S(1)}, f32[512,128]{1,0:T(8,128)S(1)}, u32[]{:S(2)}, u32[]{:S(2)}) %collective-permute-start) | collective-permute-done | bytes 262176 | tf_op jit(solution)/shard_map/ppermute | solution.py:406
  51.0 14.9 %shard_map.96 = (f32[4,16,256]{2,1,0:T(8,128)}, f32[4,16,80,256]{3,2,1,0:T(8,128)}) custom-call(s32[4,4]{1,0:T(4,128)} %block_mask_ref.3, s32[1]{0:T(128)} %bitcast.core_ref, f32[512,128]{1,0:T(8,128)S(1)} %bitcast.7, f32[512,128]{1,0:T(8,128)S(1)} %collective-permute-done.other_ref, f32[4,16,256]{2,1,0:T(8,128)} %mean_ref.1, f32[4,16,80,256]{3,2,1,0:T(8,128)} %deviation_hbm.1), custom_call_target="tpu_custom_call" | custom-call | tf_op jit(solution)/shard_map/pallas_call | solution.py:408
Async XLA Ops:
  47.3 3.7 %collective-permute-start = (f32[512,128]{1,0:T(8,128)S(1)}, f32[512,128]{1,0:T(8,128)S(1)}, u32[]{:S(2)}, u32[]{:S(2)}) collective-permute-start(f32[512,128]{1,0:T(8,128)S(1)} %bitcast.6), channel_id=1, source_target_pairs={{0,1},{1,0},{2,3},{3,2},{4,5},{5,4},{6,7},{7,6},{8,9},{9,8},{10,11... | collective-permute-start | bytes 786440 | tf_op jit(solution)/shard_map/ppermute | solution.py:406
